TPU v7x, 32 devices: a whole 2x2x4 slice. The times are simulated.
32 devices in a mesh: chan: 4 (over y, x), rows: 8 (over z, core).
Axes of the slice: x: 2, y: 2, z: 4, core: 2. Of those that a mesh axis runs over, the one named last changes fastest.
Arguments:
- residual: float32 [4, 256, 16384], P('chan', 'rows'), may hold values from -6 to 6
- psf: float32 [4, 2048, 2048], P('chan', 'rows'), may hold values from -2 to 2
- positions: int32 [32, 2], replicated, may hold values from 0 to 15360, as said below
Outputs:
- residual_out: float32 [4, 256, 16384], P('chan', 'rows')
- normalized: float32 [256, 16384], P('rows', 'chan')
Inputs may be any that keep to these rules, and one draw needn't show every extreme that they name: positions[k, 0] is a row of the image, 0 to 255; positions[k, 1] is a column from 1024 to 15360.
All inputs are finite; a program needn't handle non-finite values.
Results may differ from a plain program's by a relative error of at most 0.0001.
Values sent between devices are 32-bit elements; how exact they have to be, the bound alone decides.
A program may use at most 128 MiB of HBM per device.

v0:
```python
import functools

import jax
import jax.numpy as jnp
from jax import lax
from jax.experimental import pallas as pl
from jax.experimental.pallas import tpu as pltpu
from jax.sharding import PartitionSpec as P

STEPS = 32
LANES = 128
PIECES = 4
MESH = pl.DeviceIdType.MESH


def at(start, size):
    return pl.ds(pl.multiple_of(start, 8), size)


def aligned(row, col):
    return (pl.ds(pl.multiple_of((row >> 3) << 3, 8), 8), pl.ds(pl.multiple_of((col >> 7) << 7, LANES), LANES))


def pick(tile, row, col, lane_to, number, acc):
    moved = pltpu.roll(tile, (lane_to - col) & (LANES - 1), 1)
    return jnp.where(number == (row & 7) * LANES + lane_to, moved, acc)


def table_kernel(pos, res, psf, start, couple, tiles, psf_v, grid, pairs, load_sem, sems):
    row, nrows = lax.axis_index("rows"), lax.axis_size("rows")
    slab, steps = res.shape[1], pos.shape[1]
    shard, patch = psf.shape[1:]
    half = patch // 2
    first = row * slab
    is_root = jnp.logical_or(row == nrows // 2 - 1, row == nrows // 2)
    load = pltpu.make_async_copy(psf.at[0], psf_v, load_sem)

    @pl.when(is_root)
    def _():
        load.start()

    loads = []
    for k in range(steps):
        rows, cols = aligned(jnp.clip(pos[0, k] - first, 0, slab - 1), pos[1, k])
        loads.append(pltpu.make_async_copy(res.at[0, rows, cols], tiles.at[k], sems.at[k]))
    for copy in loads:
        copy.start()
    lane = lax.broadcasted_iota(jnp.int32, (1, LANES), 1)
    number = lax.broadcasted_iota(jnp.int32, (8, LANES), 0) * LANES + lax.broadcasted_iota(jnp.int32, (8, LANES), 1)
    peak_rows, peak_cols = jnp.zeros((1, LANES), jnp.int32), jnp.zeros((1, LANES), jnp.int32)
    for k in range(steps):
        peak_rows = jnp.where(lane == k, pos[0, k], peak_rows)
        peak_cols = jnp.where(lane == k, pos[1, k], peak_cols)
    for copy in loads:
        copy.wait()
    acc = jnp.zeros((8, LANES), jnp.float32)
    for k in range(steps):
        acc = pick(tiles[k], pos[0, k] - first, pos[1, k], k, number, acc)
    inside = (peak_rows >= first) & (peak_rows < first + slab) & (lane < steps)
    start[...] = jnp.where(inside, acc, 0.0)

    @pl.when(is_root)
    def _():
        grid[...] = jnp.zeros_like(grid)
        low = row * shard - half

        def listed(k, found):
            rk, qk = pos[0, k] - low, pos[1, k] + half

            def test(g, found):
                for i in range(8):
                    j = g * 8 + i
                    r, c = rk - pos[0, j], qk - pos[1, j]
                    owned = (r >= 0) & (r < shard) & (c >= 0) & (c < patch) & (j < k)
                    pairs[found] = k * steps + j
                    found = found + owned.astype(jnp.int32)
                return found

            return lax.fori_loop(0, (k + 7) >> 3, test, found)

        found = lax.fori_loop(0, steps, listed, jnp.int32(0))
        load.wait()

        def fill(n, carry):
            k, j = pairs[n] // steps, pairs[n] % steps
            r, c = pos[0, k] - low - pos[0, j], pos[1, k] + half - pos[1, j]
            grid[k] = pick(psf_v[aligned(r, c)], r, c, j, number, grid[k])
            return carry

        lax.fori_loop(0, found, fill, 0)
        couple[...] = jnp.sum(grid[...], axis=1)

    @pl.when(jnp.logical_not(is_root))
    def _():
        couple[...] = jnp.zeros_like(couple)


def make_tables(positions, residual, psf):
    f32 = jnp.float32
    anywhere, vmem = pl.BlockSpec(memory_space=pl.ANY), pl.BlockSpec(memory_space=pltpu.VMEM)
    return pl.pallas_call(
        table_kernel,
        out_shape=(jax.ShapeDtypeStruct((8, LANES), f32), jax.ShapeDtypeStruct((positions.shape[1], LANES), f32)),
        in_specs=[pl.BlockSpec(memory_space=pltpu.SMEM), anywhere, anywhere],
        out_specs=(vmem, vmem),
        scratch_shapes=[
            pltpu.VMEM((positions.shape[1], 8, LANES), f32), pltpu.VMEM(psf.shape[1:], f32),
            pltpu.VMEM((positions.shape[1], 8, LANES), f32), pltpu.SMEM((positions.shape[1] ** 2,), jnp.int32),
            pltpu.SemaphoreType.DMA, pltpu.SemaphoreType.DMA((positions.shape[1],)),
        ],
        name="make_tables",
    )(positions, residual, psf)


def gather_kernel(nchan, nrows, psf, start_own, couple_own, win, amps_out, psf_v, couple_in, start_in, tables, amps_v,
                  load_sem, keep_sem, send_sem, recv_sem, pass_sem, start_send, start_recv, couple_sem, table_send, table_recv, amp_send, amp_recv):
    chan, row = lax.axis_index("chan"), lax.axis_index("rows")
    chip, core = row // 2, row % 2
    partner = row + 1 - 2 * core
    nchips = nrows // 2
    slab = psf.shape[1] // nrows
    unit = 2 * slab
    low, high = nchips - 1, nchips
    steps = couple_own.shape[0]
    lane = lax.broadcasted_iota(jnp.int32, (1, LANES), 1)

    load = pltpu.make_async_copy(psf.at[0], psf_v, load_sem)
    is_low, is_high = row == low, row == high
    is_root = jnp.logical_or(is_low, is_high)

    @pl.when(is_root)
    def _():
        load.start()

    barrier = pltpu.get_barrier_semaphore()
    for step in range(1, nrows):
        pl.semaphore_signal(barrier, inc=1, device_id=(chan, (row + step) % nrows), device_id_type=MESH)
    for step in range(1, nchan):
        pl.semaphore_signal(barrier, inc=1, device_id=((chan + step) % nchan, row), device_id_type=MESH)
    pl.semaphore_wait(barrier, nrows + nchan - 2)

    def piece(to_row, z, m, h, index):
        return pltpu.make_async_remote_copy(
            src_ref=psf.at[0, pl.ds(index, slab)], dst_ref=win.at[pl.ds(m * unit + h * slab, slab)],
            send_sem=send_sem.at[z, m, h], recv_sem=recv_sem.at[m, h], device_id=(chan, to_row), device_id_type=MESH)

    def pieces(root, zs):
        out = []
        for m in range(nchips + 1):
            for z in zs:
                if (z + m < nchips) != (root == low):
                    continue
                for h in range(2):
                    to_row = root ^ 1 if z == root // 2 else 2 * z + h
                    out.append(piece(to_row, z, m, h, ((z + m) % nchips) * unit + h * slab))
        return out

    away = {low: [z for z in range(nchips) if z < low // 2], high: [z for z in range(nchips) if z > high // 2]}
    back = {low: [z for z in range(nchips) if z >= low // 2], high: [z for z in range(nchips) if z <= high // 2]}

    def kept(root):
        z = root // 2
        out = []
        for m in range(nchips + 1):
            if (z + m < nchips) == (root == low):
                out.append(pltpu.make_async_copy(psf_v.at[pl.ds(((z + m) % nchips) * unit, unit)], win.at[pl.ds(m * unit, unit)], keep_sem.at[m]))
        return out

    for root in (low, high):
        @pl.when(row == root)
        def _(root=root):
            for copy in pieces(root, away[root]):
                copy.start()

    def start_copy(source):
        return pltpu.make_async_remote_copy(
            src_ref=start_own, dst_ref=start_in.at[source], send_sem=start_send, recv_sem=start_recv.at[source],
            device_id=(chan, low), device_id_type=MESH)

    @pl.when(jnp.logical_not(is_low))
    def _():
        start_copy(row).start()

    couple_copy = pltpu.make_async_remote_copy(
        src_ref=couple_own, dst_ref=couple_in, send_sem=couple_sem.at[0], recv_sem=couple_sem.at[1],
        device_id=(chan, low), device_id_type=MESH)

    @pl.when(is_high)
    def _():
        couple_copy.start()

    for root in (low, high):
        @pl.when(row == root)
        def _(root=root):
            for copy in pieces(root, back[root]):
                copy.start()
            load.wait()
            for copy in kept(root):
                copy.start()

    def amp_copy(step):
        return pltpu.make_async_remote_copy(
            src_ref=amps_v, dst_ref=amps_v, send_sem=amp_send.at[step], recv_sem=amp_recv,
            device_id=(chan, (low + step) % nrows), device_id_type=MESH)

    def table_copy(peer, owner):
        return pltpu.make_async_remote_copy(
            src_ref=tables.at[owner], dst_ref=tables.at[owner], send_sem=table_send.at[peer], recv_sem=table_recv.at[owner],
            device_id=(peer, low), device_id_type=MESH)

    def relay(m):
        block = at(m * unit + core * slab, slab)
        return pltpu.make_async_remote_copy(
            src_ref=win.at[block], dst_ref=win.at[block], send_sem=pass_sem.at[m], recv_sem=recv_sem.at[m, core],
            device_id=(chan, partner), device_id_type=MESH)

    def arrival(m, h):
        return pltpu.make_async_remote_copy(
            src_ref=win.at[at(m * unit + h * slab, slab)], dst_ref=win.at[at(m * unit + h * slab, slab)],
            send_sem=pass_sem.at[m], recv_sem=recv_sem.at[m, h], device_id=(chan, partner), device_id_type=MESH)

    @pl.when(is_low)
    def _():
        total = start_own[...]
        for step in range(1, nrows):
            source = (low + step) % nrows
            start_copy(source).wait_recv()
            total = total + start_in[source]
        couple_copy.wait_recv()
        tables[chan, pl.ds(0, steps), :] = couple_own[...] + couple_in[...]
        tables[chan, pl.ds(steps, 8), :] = jnp.broadcast_to(jnp.sum(total, axis=0, keepdims=True), total.shape)
        for step in range(1, nchan):
            table_copy((chan + step) % nchan, chan).start()
        for step in range(1, nchan):
            table_copy((chan + step) % nchan, (chan + step) % nchan).wait_recv()
        start = jnp.concatenate([tables[c, pl.ds(steps, 1), :] for c in range(nchan)], axis=0)

        def solve(k, amps):
            couple = jnp.concatenate([tables[c, pl.ds(k, 1), :] for c in range(nchan)], axis=0)
            value = jnp.sum(jnp.where(lane == k, start, 0.0) - amps * couple, axis=1, keepdims=True)
            amp = 0.25 * (value + jnp.sum(value, axis=0, keepdims=True) / nchan)
            return jnp.where(lane == k, amp, amps)

        amps = lax.fori_loop(0, steps, solve, jnp.zeros((nchan, LANES), jnp.float32))
        amps_v[pl.ds(0, nchan), :] = amps
        amps_v[pl.ds(nchan, 8 - nchan), :] = jnp.zeros((8 - nchan, LANES), jnp.float32)
        for step in range(1, nrows):
            amp_copy(step).start()

    for m in range(nchips + 1):
        root = jnp.where(chip + m < nchips, low, high)
        relays = jnp.logical_and(row != root, partner != root)

        @pl.when(relays)
        def _(m=m):
            arrival(m, core).wait_recv()
            relay(m).start()

    for m in range(nchips + 1):
        root = jnp.where(chip + m < nchips, low, high)

        @pl.when(jnp.logical_and(row != root, partner != root))
        def _(m=m):
            arrival(m, 1 - core).wait_recv()
            relay(m).wait_send()

        @pl.when(partner == root)
        def _(m=m):
            arrival(m, 0).wait_recv()
            arrival(m, 1).wait_recv()

    for root in (low, high):
        @pl.when(row == root)
        def _(root=root):
            for copy in kept(root):
                copy.wait()
            for copy in pieces(root, away[root]) + pieces(root, back[root]):
                copy.wait_send()

    @pl.when(is_high)
    def _():
        couple_copy.wait_send()

    @pl.when(is_low)
    def _():
        for step in range(1, nchan):
            table_copy((chan + step) % nchan, chan).wait_send()
        for step in range(1, nrows):
            amp_copy(step).wait_send()

    @pl.when(jnp.logical_not(is_low))
    def _():
        start_copy(row).wait_send()
        amp_copy(1).wait_recv()

    amps_out[...] = amps_v[...]


def gather_patch(nchan, nrows, psf, start, couple):
    shard, patch = psf.shape[1:]
    steps, slab = couple.shape[0], shard // nrows
    nchips = nrows // 2
    rows = slab * (nrows + 2)
    dma, f32 = pltpu.SemaphoreType.DMA, jnp.float32
    anywhere = pl.BlockSpec(memory_space=pl.ANY)
    return pl.pallas_call(
        functools.partial(gather_kernel, nchan, nrows),
        out_shape=(jax.ShapeDtypeStruct((rows, patch), f32), jax.ShapeDtypeStruct((8, LANES), f32)),
        in_specs=[anywhere, pl.BlockSpec(memory_space=pltpu.VMEM), pl.BlockSpec(memory_space=pltpu.VMEM)],
        out_specs=(anywhere, pl.BlockSpec(memory_space=pltpu.VMEM)),
        scratch_shapes=[
            pltpu.VMEM((shard, patch), f32), pltpu.VMEM((steps, LANES), f32), pltpu.VMEM((nrows, 8, LANES), f32),
            pltpu.VMEM((nchan, steps + 8, LANES), f32), pltpu.VMEM((8, LANES), f32),
            dma, dma((nchips + 1,)), dma((nchips, nchips + 1, 2)), dma((nchips + 1, 2)), dma((nchips + 1,)),
            dma, dma((nrows,)), dma((2,)), dma((nchan,)), dma((nchan,)), dma((nrows,)), dma,
        ],
        compiler_params=pltpu.CompilerParams(collective_id=0, has_side_effects=True),
        name="gather_patch",
    )(psf, start, couple)


def apply_kernel(pos, amps, res, win, out, image, patch_v, sems):
    chan, row = lax.axis_index("chan"), lax.axis_index("rows")
    nrows = lax.axis_size("rows")
    slab, ncols = res.shape[1], res.shape[2]
    rows, patch = win.shape
    chunks = patch // LANES
    tiles = slab // 8
    loads = [pltpu.make_async_copy(win.at[:, pl.ds(c * LANES, LANES)], patch_v.at[c], sems.at[c]) for c in range(chunks)]

    def band(t):
        return pltpu.make_async_copy(res.at[0, pl.ds(8 * t, 8)], image.at[pl.ds(8 * t, 8), pl.ds(0, ncols)], sems.at[chunks + t])

    def done(t):
        return pltpu.make_async_copy(image.at[pl.ds(8 * t, 8), pl.ds(0, ncols)], out.at[0, pl.ds(8 * t, 8)], sems.at[chunks + tiles + t])

    band(0).start()
    for copy in loads:
        copy.start()
    for t in range(1, tiles):
        band(t).start()
    for copy in loads:
        copy.wait()
    lane = lax.broadcasted_iota(jnp.int32, (8, LANES), 1)
    top = (row % 2) * slab + slab * nrows

    zero = jnp.zeros((8, LANES), jnp.float32)
    for pair in range(tiles // 2):
        mine = (2 * pair, 2 * pair + 1)
        for t in mine:
            band(t).wait()

        def step(k, carry, mine=mine):
            amp = amps[chan, k]
            begin = top - pos[0, k]
            left = pos[1, k] - patch // 2
            shift = left & (LANES - 1)
            span = pl.ds(pl.multiple_of(left - shift, LANES), patch + LANES)
            keep = lane < shift
            for t in mine:
                moved = [zero] + [pltpu.roll(patch_v[c, pl.ds(begin + 8 * t, 8), :] * amp, shift, 1) for c in range(chunks)] + [zero]
                change = jnp.concatenate([jnp.where(keep, moved[c], moved[c + 1]) for c in range(chunks + 1)], axis=1)
                image[pl.ds(8 * t, 8), span] = image[pl.ds(8 * t, 8), span] - change
            return carry

        lax.fori_loop(0, pos.shape[1], step, 0)
        for t in mine:
            done(t).start()
    for t in range(tiles):
        done(t).wait()


def apply_peaks(positions, amps, residual, win):
    slab, ncols = residual.shape[1:]
    rows, patch = win.shape
    chunks = patch // LANES
    anywhere, scalars = pl.BlockSpec(memory_space=pl.ANY), pl.BlockSpec(memory_space=pltpu.SMEM)
    return pl.pallas_call(
        apply_kernel,
        out_shape=jax.ShapeDtypeStruct(residual.shape, jnp.float32),
        in_specs=[scalars, scalars, anywhere, anywhere],
        out_specs=anywhere,
        scratch_shapes=[
            pltpu.VMEM((slab, ncols + LANES), jnp.float32), pltpu.VMEM((chunks, rows, LANES), jnp.float32),
            pltpu.SemaphoreType.DMA((chunks + slab // 4,)),
        ],
        name="apply_peaks",
    )(positions, amps, residual, win)


def sum_kernel(nchan, nrows, image, out, total_out, own, near, first_far, first_own, passed, second, squares,
               load_sem, far_send, far_recv, own_send, own_recv, pass_send, pass_recv, square_send, square_recv):
    chan, row = lax.axis_index("chan"), lax.axis_index("rows")
    me = row * nchan + chan
    slab, ncols = image.shape[1], image.shape[2]
    cols = ncols // nchan
    part = slab // 2
    width = cols // PIECES
    bits = ((1, 2), (2, 1))

    def block(c):
        return pl.ds(pl.multiple_of(c * cols, LANES), cols)

    def flip(bit):
        if bit == 1:
            return chan + 1 - 2 * (chan % 2)
        return (chan + 2) % 4

    diagonal = 3 - chan
    loads = [pltpu.make_async_copy(image.at[0, :, block(chan)], own, load_sem.at[0])]
    for p in range(2):
        loads.append(pltpu.make_async_copy(image.at[0, pl.ds(p * part, part), block(flip(bits[p][1]))], near.at[p], load_sem.at[1 + p]))
    for copy in loads:
        copy.start()

    barrier = pltpu.get_barrier_semaphore()
    for step in range(1, nrows * nchan):
        other = (me + step) % (nrows * nchan)
        pl.semaphore_signal(barrier, inc=1, device_id=(other % nchan, other // nchan), device_id_type=MESH)
    pl.semaphore_wait(barrier, nrows * nchan - 1)

    def send(p, g, source, dest, send_sem, recv_sem, to):
        return pltpu.make_async_remote_copy(
            src_ref=source, dst_ref=dest.at[p, :, pl.ds(g * width, width)], send_sem=send_sem.at[p, g], recv_sem=recv_sem.at[p, g],
            device_id=(to, row), device_id_type=MESH)

    def tile(p, g, c):
        return image.at[0, pl.ds(p * part, part), pl.ds(pl.multiple_of(c * cols + g * width, LANES), width)]

    def far(p, g):
        return send(p, g, tile(p, g, diagonal), first_far, far_send, far_recv, flip(bits[p][0]))

    def mine(p, g):
        return send(p, g, tile(p, g, flip(bits[p][0])), first_own, own_send, own_recv, flip(bits[p][0]))

    def onward(p, g):
        return send(p, g, passed.at[p, :, pl.ds(g * width, width)], second, pass_send, pass_recv, flip(bits[p][1]))

    for g in range(PIECES):
        for p in range(2):
            far(p, g).start()
    for g in range(PIECES):
        for p in range(2):
            mine(p, g).start()
    for copy in loads:
        copy.wait()
    for g in range(PIECES):
        for p in range(2):
            span = pl.ds(g * width, width)
            far(p, g).wait_recv()
            passed[p, :, span] = near[p, :, span] + first_far[p, :, span]
            onward(p, g).start()
    for g in range(PIECES):
        for p in range(2):
            span = pl.ds(g * width, width)
            mine(p, g).wait_recv()
            rows = pl.ds(p * part, part)
            own[rows, span] = own[rows, span] + first_own[p, :, span]
    total = jnp.zeros((8, LANES), jnp.float32)
    for g in range(PIECES):
        for p in range(2):
            span = pl.ds(g * width, width)
            onward(p, g).wait_recv()
            rows = pl.ds(p * part, part)
            value = own[rows, span] + second[p, :, span]
            own[rows, span] = value
            square = value * value
            for t in range(part // 8):
                for c in range(width // LANES):
                    total = total + square[8 * t:8 * t + 8, c * LANES:(c + 1) * LANES]
    squares[pl.ds(me, 1), :] = jnp.sum(total, axis=0, keepdims=True)

    def spread(step):
        other = (me + step) % (nrows * nchan)
        return pltpu.make_async_remote_copy(
            src_ref=squares.at[pl.ds(me, 1)], dst_ref=squares.at[pl.ds(me, 1)], send_sem=square_send.at[step], recv_sem=square_recv.at[step],
            device_id=(other % nchan, other // nchan), device_id_type=MESH)

    def arrived(step):
        other = (me + nrows * nchan - step) % (nrows * nchan)
        return pltpu.make_async_remote_copy(
            src_ref=squares.at[pl.ds(other, 1)], dst_ref=squares.at[pl.ds(other, 1)], send_sem=square_send.at[step], recv_sem=square_recv.at[step],
            device_id=(other % nchan, other // nchan), device_id_type=MESH)

    for step in range(1, nrows * nchan):
        spread(step).start()
    keep = pltpu.make_async_copy(own, out, load_sem.at[0])
    keep.start()
    for step in range(1, nrows * nchan):
        arrived(step).wait_recv()
    everything = jnp.sum(jnp.sum(squares[...], axis=0, keepdims=True), axis=1, keepdims=True)
    total_out[...] = jnp.broadcast_to(everything, total_out.shape)
    keep.wait()
    for step in range(1, nrows * nchan):
        spread(step).wait_send()
    for g in range(PIECES):
        for p in range(2):
            far(p, g).wait_send()
            mine(p, g).wait_send()
            onward(p, g).wait_send()


def sum_channels(nchan, nrows, image):
    slab, ncols = image.shape[1:]
    cols, part = ncols // nchan, slab // 2
    dma, f32 = pltpu.SemaphoreType.DMA, jnp.float32
    halves = pltpu.VMEM((2, part, cols), f32)
    parts, total = pl.pallas_call(
        functools.partial(sum_kernel, nchan, nrows),
        out_shape=(jax.ShapeDtypeStruct((slab, cols), f32), jax.ShapeDtypeStruct((8, LANES), f32)),
        in_specs=[pl.BlockSpec(memory_space=pl.ANY)],
        out_specs=(pl.BlockSpec(memory_space=pl.ANY), pl.BlockSpec(memory_space=pltpu.VMEM)),
        scratch_shapes=[pltpu.VMEM((slab, cols), f32)] + [halves] * 5 + [pltpu.VMEM((nrows * nchan, LANES), f32), dma((3,))]
        + [dma((2, PIECES))] * 6 + [dma((nrows * nchan,))] * 2,
        compiler_params=pltpu.CompilerParams(collective_id=1, has_side_effects=True),
        name="sum_channels",
    )(image)
    return parts * lax.rsqrt(total[0, 0] / (slab * nrows * ncols) + 1e-06)


def on_device(residual, psf, positions):
    nchan, nrows = lax.axis_size("chan"), lax.axis_size("rows")
    slab, ncols = residual.shape[1:]
    shard, patch = psf.shape[1:]
    central = nrows % 2 == 0 and slab * nrows == shard and 2 * shard * (nrows // 2) == patch
    powers = shard & (shard - 1) == 0 and patch & (patch - 1) == 0
    if not (central and powers and nchan == 4 and slab % 16 == 0 and positions.shape[0] % 8 == 0 and positions.shape[0] <= LANES):
        return on_any_device(residual, psf, positions)
    positions = positions.T
    start, couple = make_tables(positions, residual, psf)
    win, amps = gather_patch(nchan, nrows, psf, start, couple)
    image = apply_peaks(positions, amps, residual, win)
    return (image, sum_channels(nchan, nrows, image))


def on_any_device(residual, psf, positions):
    chan_id = lax.axis_index("chan")
    nchan = lax.axis_size("chan")
    row_id = lax.axis_index("rows")
    nrows = lax.axis_size("rows")
    slab = residual.shape[1]
    ncols = residual.shape[2]
    own_psf = psf[0]
    shard_rows = own_psf.shape[0]
    patch = own_psf.shape[1]
    half = patch // 2
    first = row_id * slab
    chan_hot = (jnp.arange(nchan) == chan_id).astype(jnp.float32)
    full_psf = lax.all_gather(own_psf, "rows", axis=0, tiled=True)
    padded_psf = jnp.pad(full_psf, ((slab, slab), (0, 0)))
    zero = jnp.int32(0)

    def subtract(image, row, col, amount):
        offset = first - row + half
        touches = jnp.logical_and(offset > -slab, offset < patch)
        start = jnp.clip(offset + slab, 0, patch + slab)
        psf_rows = lax.dynamic_slice(padded_psf, (start, zero), (slab, patch))
        window = lax.dynamic_slice(image, (zero, col - half), (slab, patch))
        scale = jnp.where(touches, amount, 0.0)
        return lax.dynamic_update_slice(image, window - scale * psf_rows, (zero, col - half))

    image = residual[0]
    peak_rows = positions[:, 0]
    peak_cols = positions[:, 1]
    inside = jnp.logical_and(peak_rows >= first, peak_rows < first + slab)
    local_rows = jnp.clip(peak_rows - first, 0, slab - 1)
    start_values = jnp.where(inside, image[local_rows, peak_cols], 0.0)
    row_offset = peak_rows[:, None] - peak_rows[None, :] + half - row_id * shard_rows
    col_offset = peak_cols[:, None] - peak_cols[None, :] + half
    owned = (row_offset >= 0) & (row_offset < shard_rows) & (col_offset >= 0) & (col_offset < patch)
    couple = own_psf[jnp.clip(row_offset, 0, shard_rows - 1), jnp.clip(col_offset, 0, patch - 1)]
    couple = jnp.where(owned, couple, 0.0)
    start_table, couple_table = lax.psum(
        (chan_hot[:, None] * start_values[None, :], chan_hot[:, None, None] * couple[None, :, :]),
        ("chan", "rows"),
    )

    def solve(k, amps):
        taken = jnp.sum(amps * lax.dynamic_index_in_dim(couple_table, k, 1, False), axis=1)
        value = lax.dynamic_index_in_dim(start_table, k, 1, False) - taken
        amp = 0.25 * (value + jnp.sum(value) / nchan)
        return lax.dynamic_update_index_in_dim(amps, amp, k, 1)

    amps = lax.fori_loop(0, STEPS, solve, jnp.zeros((nchan, STEPS), jnp.float32))
    own_amps = jnp.sum(chan_hot[:, None] * amps, axis=0)

    def apply(k, image):
        return subtract(image, positions[k, 0], positions[k, 1], own_amps[k])

    image = lax.fori_loop(0, STEPS, apply, image)
    count = slab * nrows * ncols
    parts = lax.psum_scatter(image, "chan", scatter_dimension=1, tiled=True)
    total = lax.psum(jnp.sum(parts * parts), ("chan", "rows"))
    normalized = parts * lax.rsqrt(total / count + 1e-06)
    return (image[None], normalized)


def solution(mesh):
    return jax.shard_map(
        on_device,
        mesh=mesh,
        in_specs=(P("chan", "rows", None), P("chan", "rows", None), P()),
        out_specs=(P("chan", "rows", None), P("rows", "chan")),
        check_vma=False,
    )
```

profile of v0, /device:TPU:0, one launch (start us, length us, event | category | flops | bytes accessed | tf_op | source)
XLA Modules:
  0.0 92.6 jit_solution(15623742310056886061)
XLA Ops:
  0.6 2.7 %make_tables.1 = (f32[8,128]{1,0:T(8,128)}, f32[32,128]{1,0:T(8,128)}) custom-call(s32[2,32]{1,0:T(2,128)} %bitcast.2, f32[1,32,16384]{2,1,0:T(8,128)} %res.3, f32[1,256,2048]{2,1,0:T(8,128)} %psf.3), custom_call_target="tpu_custom_call" | custom-call | tf_op jit(solution)/shard_map/make_tables/pallas_call | solution.py:101
  3.3 46.2 %gather_patch.1 = (f32[320,2048]{1,0:T(8,128)}, f32[8,128]{1,0:T(8,128)}) custom-call(f32[1,256,2048]{2,1,0:T(8,128)} %psf.3, f32[8,128]{1,0:T(8,128)} %get-tuple-element.8.start_own, f32[32,128]{1,0:T(8,128)} %get-tuple-element.9.couple_own), custom_call_target="tpu_custom_call" | custom-call | tf_op jit(solution)/shard_map/gather_patch/pallas_call | solution.py:306
  49.6 10.7 %apply_peaks.1.image = f32[1,32,16384]{2,1,0:T(8,128)} custom-call(s32[2,32]{1,0:T(2,128)} %bitcast.3, f32[8,128]{1,0:T(8,128)} %get-tuple-element.10.amps, f32[1,32,16384]{2,1,0:T(8,128)} %res.3, f32[320,2048]{1,0:T(8,128)} %get-tuple-element.11.win), custom_call_target="tpu_custom_call" | custom-call | tf_op jit(solution)/shard_map/apply_peaks/pallas_call | solution.py:378
  60.2 28.6 %sum_channels.1 = (f32[32,4096]{1,0:T(8,128)}, f32[8,128]{1,0:T(8,128)}) custom-call(f32[1,32,16384]{2,1,0:T(8,128)} %apply_peaks.1.image), custom_call_target="tpu_custom_call" | custom-call | tf_op jit(solution)/shard_map/sum_channels/pallas_call | solution.py:508
  88.8 1.2 %slice.3 = f32[1,1]{1,0:T(1,128)} slice(f32[8,128]{1,0:T(8,128)} %get-tuple-element.13), slice={[0:1], [0:1]} | slice | bytes 8 | tf_op jit(solution)/shard_map/slice | solution.py:518
  90.7 1.9 %broadcast_multiply_fusion = f32[32,4096]{1,0:T(8,128)} fusion(f32[32,4096]{1,0:T(8,128)} %get-tuple-element.12, f32[]{:T(128)} %bitcast.1), kind=kLoop, calls=%fused_computation | loop fusion | flops 131072 | bytes 1048580 | tf_op jit(solution)/shard_map/mul | solution.py:518
where the time goes:
time: 93.2 us; the launch traced here: 92.6 us
  Pallas kernels  88.2 us (95%)
  other arithmetic  1.87 us (2%)
  between operations  1.35 us (1%)
  local copies, waits for them, and re-layouts  1.19 us (1%)
    pallas_call x1, Pallas kernels, gather_patch(): pl.pallas_call(functools.partial(gather_kernel, nchan, nrows), out_shape=...  46.2 us
    pallas_call x1, Pallas kernels, sum_channels(): pl.pallas_call(functools.partial(sum_kernel, nchan, nrows), out_shape=(ja...  28.6 us
    pallas_call x1, Pallas kernels, apply_peaks(): pl.pallas_call(apply_kernel, out_shape=jax.ShapeDtypeStruct(residual.shap...  10.7 us
    pallas_call x1, Pallas kernels, make_tables(): pl.pallas_call(table_kernel, out_shape=(jax.ShapeDtypeStruct((8, LANES),...  2.66 us
    mul x1, other arithmetic, sum_channels(): return parts * lax.rsqrt(total[0, 0] / (slab * nrows * ncols) + 1e-06)  1.87 us

commit v1 on v0

v1 whole, which is shorter than its diff:
```python
import functools

import jax
import jax.numpy as jnp
from jax import lax
from jax.experimental import pallas as pl
from jax.experimental.pallas import tpu as pltpu
from jax.sharding import PartitionSpec as P

STEPS = 32
LANES = 128
MESH = pl.DeviceIdType.MESH
OUT = pltpu.VMEM


def pick(tile, row, col, lane_to, owned, number, acc):
    moved = pltpu.roll(tile, (lane_to - col) & (LANES - 1), 1)
    target = jnp.where(owned, (row & 7) * LANES + lane_to, -1)
    return jnp.where(number == target, moved, acc)


def cycle_kernel(nchan, nrows, pos, res, psf, image, parts, total_out,
                 work, land, patch_v, psf_v, grid, couple_v, couple_in, start_v, start_in, tables, amps_v, prev_v, last_v,
                 first_far, first_own, passed, second, squares, prev_s, last_s, amps_s,
                 ready, band_sem, psf_sem, index_sem, send_sem, unit_recv, recv_sem, relay_sem, fine_send, fine_recv, fine_relay,
                 start_send, start_recv, couple_send, couple_recv, table_send, table_recv, amp_send, amp_recv,
                 far_send, far_recv, own_send, own_recv, pass_send, pass_recv, square_send, square_recv):
    chan, row = lax.axis_index("chan"), lax.axis_index("rows")
    chip, core = row // 2, row % 2
    partner = row + 1 - 2 * core
    nchips = nrows // 2
    side = chip // (nchips // 2)
    slab, ncols = res.shape[1], res.shape[2]
    shard, patch = psf.shape[1:]
    half, steps, chunks = patch // 2, pos.shape[1], patch // LANES
    unit, tiles, blocks = 2 * slab, slab // 8, ncols // LANES
    base, width = blocks + 1, chunks + 1
    first = row * slab
    roots = (nchips - 1, nchips)
    solvers = (roots[0] ^ 1, roots[1] ^ 1)
    is_root = jnp.logical_or(row == roots[0], row == roots[1])
    is_solver = jnp.logical_or(row == solvers[0], row == solvers[1])
    is_mid = jnp.logical_or(is_root, is_solver)
    is_end = jnp.logical_not(is_mid)
    lane = lax.broadcasted_iota(jnp.int32, (1, LANES), 1)
    lane8 = lax.broadcasted_iota(jnp.int32, (8, LANES), 1)
    number = lax.broadcasted_iota(jnp.int32, (8, LANES), 0) * LANES + lane8
    zero = jnp.zeros((8, LANES), jnp.float32)

    def block_at(index):
        return pl.ds(pl.multiple_of(index * LANES, LANES), LANES)

    bands = [pltpu.make_async_copy(res.at[0, pl.ds(8 * t, 8)], image.at[pl.ds(8 * t, 8)], band_sem.at[t]) for t in range(tiles)]
    for copy in bands:
        copy.start()
    loads = [pltpu.make_async_copy(psf.at[0, :, pl.ds(c * LANES, LANES)], psf_v.at[c], psf_sem.at[c]) for c in range(chunks)]

    barrier = pltpu.get_barrier_semaphore()
    for step in range(1, nrows):
        pl.semaphore_signal(barrier, inc=1, device_id=(chan, (row + step) % nrows), device_id_type=MESH)
    for step in range(1, nchan):
        pl.semaphore_signal(barrier, inc=1, device_id=((chan + step) % nchan, row), device_id_type=MESH)

    @pl.when(is_root)
    def _():
        for copy in loads:
            copy.start()

    begins = [jnp.clip(pos[1, k] - half, 0, ncols - patch) >> 7 for k in range(steps)]
    krow = lax.broadcasted_iota(jnp.int32, (steps, LANES), 0)
    target = jnp.zeros((steps, LANES), jnp.int32)
    for k in range(steps):
        target = jnp.where(krow == k, begins[k], target)
    target = target + lax.broadcasted_iota(jnp.int32, (steps, LANES), 1)
    prev, last = target, lane8
    for k in range(steps):
        inside = target - begins[k]
        prev = jnp.where((inside >= 0) & (inside < width) & (krow > k), inside + (base + width * k), prev)
        inside = lane8 - begins[k]
        last = jnp.where((inside >= 0) & (inside < width), inside + (base + width * k), last)
    prev_v[...] = prev
    last_v[...] = last
    index_copies = [pltpu.make_async_copy(prev_v, prev_s, index_sem.at[0]), pltpu.make_async_copy(last_v, last_s, index_sem.at[1])]
    for copy in index_copies:
        copy.start()
    for t in range(tiles):
        work[t, blocks] = zero
    pl.semaphore_wait(barrier, nrows + nchan - 2)

    def bulk(s):
        mid, end, other = (nchips - 1 + s) // 2, (nchips - 1) * s, nchips // 2 - s
        order = (0, 1) if s == 0 else (1, 0)
        near = list(range(nchips)) if s == 0 else list(range(2 * nchips - 1, nchips - 1, -1))
        across = [nchips - 1 - n if s == 0 else nchips + n for n in range(nchips // 2)]
        local = [u for u in range(mid, mid + nchips + 1) if (u < nchips) == (s == 0)]
        out = []

        def add(u, z, h, rows, to_row, sem):
            out.append(pltpu.make_async_remote_copy(
                src_ref=psf.at[0, pl.ds((u % nchips) * unit + h * slab, rows)], dst_ref=land.at[pl.ds((u - z) * unit + h * slab, rows)],
                send_sem=send_sem.at[len(out)], recv_sem=sem, device_id=(chan, to_row), device_id_type=MESH))

        for u in near:
            for h in order:
                add(u, end, h, slab, 2 * end + h, recv_sem.at[u - end, h])
        for u in across:
            for h in range(2):
                add(u, other, h, slab, 2 * other + h, recv_sem.at[u - other, h])
        for u in local:
            add(u, mid, 0, unit, solvers[s], unit_recv.at[u - mid])
        return out

    for s in range(2):
        @pl.when(row == roots[s])
        def _(s=s):
            for copy in bulk(s):
                copy.start()

    for step in range(1, nchan):
        pl.semaphore_signal(ready, inc=1, device_id=((chan + step) % nchan, row), device_id_type=MESH)

    for copy in bands:
        copy.wait()

    def spread_out(b, carry):
        for t in range(tiles):
            work[t, b] = image[pl.ds(8 * t, 8), block_at(b)]
        return carry

    lax.fori_loop(0, blocks, spread_out, 0, unroll=4)
    acc = zero
    for k in range(steps):
        r, c = pos[0, k] - first, pos[1, k]
        tile = work[(r >> 3) & (tiles - 1), c >> 7]
        acc = pick(tile, r, c, k, (r >= 0) & (r < slab), number, acc)
    start_v[...] = acc

    def start_copy(s, source):
        return pltpu.make_async_remote_copy(
            src_ref=start_v, dst_ref=start_in.at[source], send_sem=start_send, recv_sem=start_recv.at[source],
            device_id=(chan, solvers[s]), device_id_type=MESH)

    def couple_copy(s):
        return pltpu.make_async_remote_copy(
            src_ref=couple_v, dst_ref=couple_in, send_sem=couple_send, recv_sem=couple_recv,
            device_id=(chan, solvers[s]), device_id_type=MESH)

    for s in range(2):
        @pl.when((side == s) & (row != solvers[s]))
        def _(s=s):
            start_copy(s, row).start()

    @pl.when(is_root)
    def _():
        for copy in loads:
            copy.wait()
        low = row * shard - half

        def fill(k, carry):
            rk, qk = pos[0, k] - low, pos[1, k] + half

            def test(g, acc):
                for i in range(8):
                    j = g * 8 + i
                    r, c = rk - pos[0, j], qk - pos[1, j]
                    owned = (r >= 0) & (r < shard) & (c >= 0) & (c < patch) & (j < k)
                    tile = psf_v[(c >> 7) & (chunks - 1), pl.ds(((r >> 3) << 3) & (shard - 1), 8), :]
                    acc = pick(tile, r, c, j, owned, number, acc)
                return acc

            grid[k] = lax.fori_loop(0, (k + 7) >> 3, test, zero)
            return carry

        lax.fori_loop(0, steps, fill, 0)
        couple_v[...] = jnp.sum(grid[...], axis=1)

    for s in range(2):
        @pl.when(row == roots[s])
        def _(s=s):
            couple_copy(s).start()

    def held(m, h, rows=slab):
        return land.at[pl.ds(pl.multiple_of(m * unit + h * slab, 8), rows)]

    def relay(m):
        return pltpu.make_async_remote_copy(
            src_ref=held(m, core), dst_ref=held(m, core), send_sem=relay_sem.at[m], recv_sem=recv_sem.at[m, core],
            device_id=(chan, partner), device_id_type=MESH)

    def arrival(m, h):
        return pltpu.make_async_remote_copy(
            src_ref=held(m, h), dst_ref=held(m, h), send_sem=relay_sem.at[m], recv_sem=recv_sem.at[m, h],
            device_id=(chan, partner), device_id_type=MESH)

    def pass_on(m):
        arrival(m, core).wait_recv()
        relay(m).start()

    def crossed(n):
        return jnp.where(side == 0, nchips - 1 + n, 1 - n)

    def streamed(n):
        return jnp.where(side == 0, n, nchips - n)

    def relayout(source, source_row, dest_row, rows):
        def body(g, carry):
            take, put = pl.multiple_of(source_row + 8 * g, 8), pl.multiple_of(dest_row + 8 * g, 8)
            for c in range(chunks):
                tile = source[c, pl.ds(take, 8), :] if len(source.shape) == 3 else source[pl.ds(take, 8), pl.ds(c * LANES, LANES)]
                patch_v[c, pl.ds(put, 8), :] = tile
            return carry

        lax.fori_loop(0, rows // 8, body, 0)

    @pl.when(is_mid)
    def _():
        pass_on(crossed(0))

    pl.semaphore_wait(ready, nchan - 1)
    me_table = 2 * chan + side

    def table_copy(step):
        other = (me_table + step) % (2 * nchan)
        return pltpu.make_async_remote_copy(
            src_ref=tables.at[me_table], dst_ref=tables.at[me_table], send_sem=table_send.at[step], recv_sem=table_recv.at[step],
            device_id=(other // 2, solvers[0] + (other % 2) * (solvers[1] - solvers[0])), device_id_type=MESH)

    def table_arrival(step):
        other = (me_table + 2 * nchan - step) % (2 * nchan)
        return pltpu.make_async_remote_copy(
            src_ref=tables.at[other], dst_ref=tables.at[other], send_sem=table_send.at[step], recv_sem=table_recv.at[step],
            device_id=(other // 2, solvers[0] + (other % 2) * (solvers[1] - solvers[0])), device_id_type=MESH)

    for s in range(2):
        @pl.when(row == solvers[s])
        def _(s=s):
            total = start_v[...]
            for source in range(s * nchips, (s + 1) * nchips):
                if source != solvers[s]:
                    start_copy(s, source).wait_recv()
                    total = total + start_in[source]
            couple_copy(s).wait_recv()
            tables[me_table, pl.ds(0, steps), :] = couple_in[...]
            tables[me_table, pl.ds(steps, 8), :] = jnp.broadcast_to(jnp.sum(total, axis=0, keepdims=True), total.shape)
            for step in range(1, 2 * nchan):
                table_copy(step).start()

    @pl.when(is_mid)
    def _():
        pass_on(crossed(1))

    def amp_copy(n):
        return pltpu.make_async_remote_copy(
            src_ref=amps_v, dst_ref=amps_v, send_sem=amp_send.at[n], recv_sem=amp_recv,
            device_id=(chan, side * nchips + (row + n) % nchips), device_id_type=MESH)

    @pl.when(is_solver)
    def _():
        for step in range(1, 2 * nchan):
            table_arrival(step).wait_recv()

        def rows_of(index):
            return jnp.concatenate([tables[2 * c, pl.ds(index, 1), :] + tables[2 * c + 1, pl.ds(index, 1), :] for c in range(nchan)], axis=0)

        start = rows_of(steps)

        def solve(k, amps):
            value = jnp.sum(jnp.where(lane == k, start, 0.0) - amps * rows_of(k), axis=1, keepdims=True)
            amp = 0.25 * (value + jnp.sum(value, axis=0, keepdims=True) / nchan)
            return jnp.where(lane == k, amp, amps)

        amps = lax.fori_loop(0, steps, solve, jnp.zeros((nchan, LANES), jnp.float32))
        amps_v[pl.ds(0, nchan), :] = amps
        amps_v[pl.ds(nchan, 8 - nchan), :] = jnp.zeros((8 - nchan, LANES), jnp.float32)
        for n in range(1, nchips):
            amp_copy(n).start()

    def fine_piece(n):
        return jnp.where(side == 0, n, 2 * tiles - 1 - n)

    def fine_at(n):
        return pl.multiple_of(jnp.where(side == 0, nchips, 0) * unit + 8 * fine_piece(n), 8)

    def onward_piece(s, n):
        mid, end = (nchips - 1 + s) // 2, (nchips - 1) * s
        u = nchips - s
        j = n if s == 0 else 2 * tiles - 1 - n
        return pltpu.make_async_remote_copy(
            src_ref=land.at[pl.ds((u - mid) * unit + 8 * j, 8)], dst_ref=land.at[pl.ds((u - end) * unit + 8 * j, 8)],
            send_sem=fine_send.at[n], recv_sem=fine_recv.at[n], device_id=(chan, 2 * end + j // tiles), device_id_type=MESH)

    def fine_copy(n):
        return pltpu.make_async_remote_copy(
            src_ref=land.at[pl.ds(fine_at(n), 8)], dst_ref=land.at[pl.ds(fine_at(n), 8)],
            send_sem=fine_relay.at[n], recv_sem=fine_recv.at[n], device_id=(chan, partner), device_id_type=MESH)

    for s in range(2):
        mid = (nchips - 1 + s) // 2
        local = [u for u in range(mid, mid + nchips + 1) if (u < nchips) == (s == 0)]

        @pl.when(row == roots[s])
        def _(s=s, mid=mid, local=local):
            arrival(crossed(0), 1 - core).wait_recv()
            for n in range(2 * tiles):
                onward_piece(s, n).start()
            relayout(psf_v, (local[0] % nchips) * unit, (local[0] - mid) * unit, len(local) * unit)

        @pl.when(row == solvers[s])
        def _(s=s, mid=mid, local=local):
            arrival(crossed(0), 1 - core).wait_recv()
            for u in local:
                pltpu.make_async_remote_copy(
                    src_ref=held(u - mid, 0, unit), dst_ref=held(u - mid, 0, unit), send_sem=send_sem.at[0], recv_sem=unit_recv.at[u - mid],
                    device_id=(chan, partner), device_id_type=MESH).wait_recv()
            relayout(land, (local[0] - mid) * unit, (local[0] - mid) * unit, len(local) * unit)

    @pl.when(is_mid)
    def _():
        arrival(crossed(1), 1 - core).wait_recv()
        begin = jnp.where(side == 0, nchips - 1, 0) * unit
        relayout(land, begin, begin, 2 * unit)

    @pl.when(is_end)
    def _():
        for n in range(nchips):
            pass_on(streamed(n))
        for n in range(nchips):
            arrival(streamed(n), 1 - core).wait_recv()
        begin = jnp.where(side == 0, 0, 1) * unit
        relayout(land, begin, begin, nchips * unit)

    @pl.when(jnp.logical_not(is_solver))
    def _():
        amp_copy(1).wait_recv()

    amps_copy = pltpu.make_async_copy(amps_v, amps_s, index_sem.at[2])
    amps_copy.start()
    for copy in index_copies:
        copy.wait()
    amps_copy.wait()

    leading = core == side
    cols = ncols // nchan
    span = cols // 2
    bits = ((1, 2), (2, 1))
    top = core * slab + slab * nrows

    def flip(bit):
        if bit == 1:
            return chan + 1 - 2 * (chan % 2)
        return (chan + 2) % 4

    diagonal = 3 - chan

    def tile_at(i):
        return jnp.where(side == 0, i, tiles - 1 - i)

    def rows_at(i):
        return pl.ds(pl.multiple_of(8 * tile_at(i), 8), 8)

    def cols_at(c, p):
        return pl.ds(pl.multiple_of(c * cols + p * span, LANES), span)

    def send(i, p, source, dest, send_sem, recv_sem, to):
        return pltpu.make_async_remote_copy(
            src_ref=source, dst_ref=dest.at[i, p], send_sem=send_sem.at[i, p], recv_sem=recv_sem.at[i, p],
            device_id=(to, row), device_id_type=MESH)

    def far(i, p):
        return send(i, p, image.at[rows_at(i), cols_at(diagonal, p)], first_far, far_send, far_recv, flip(bits[p][0]))

    def mine(i, p):
        return send(i, p, image.at[rows_at(i), cols_at(flip(bits[p][0]), p)], first_own, own_send, own_recv, flip(bits[p][0]))

    def onward(i, p):
        return send(i, p, passed.at[i, p], second, pass_send, pass_recv, flip(bits[p][1]))

    def fetch(n):
        fine_copy(n).wait_recv()

    def pieces_for(i):
        @pl.when(is_end & leading)
        def _():
            fetch(i)
            fine_copy(i).start()
            relayout(land, fine_at(i), fine_at(i), 8)

        @pl.when(is_end & jnp.logical_not(leading))
        def _():
            for n in (range(tiles + 1) if i == 0 else (tiles + i,)):
                fetch(n)
                relayout(land, fine_at(n), fine_at(n), 8)

    def apply(i):
        t = tile_at(i)
        lift = top + 8 * t

        def two(kk, carry):
            for k in (2 * kk, 2 * kk + 1):
                amp = amps_s[chan, k]
                begin = lift - pos[0, k]
                shift = (pos[1, k] - half) & (LANES - 1)
                keep = lane8 < shift
                moved = [zero] + [pltpu.roll(patch_v[c, pl.ds(begin, 8), :] * amp, shift, 1) for c in range(chunks)] + [zero]
                for m in range(width):
                    change = jnp.where(keep, moved[m], moved[m + 1])
                    work[t, base + width * k + m] = work[t, prev_s[k, m]] - change
            return carry

        lax.fori_loop(0, steps // 2, two, 0)

    def finalize(i, c):
        rows = rows_at(i)
        per = cols // LANES

        def body(g, carry):
            for n in range(8):
                b = c * per + g * 8 + n
                image[rows, block_at(b)] = work[tile_at(i), last_s[0, b]]
            return carry

        lax.fori_loop(0, per // 8, body, 0)

    def combine(i):
        for p in range(2):
            far(i, p).wait_recv()
            passed[i, p] = image[rows_at(i), cols_at(flip(bits[p][1]), p)] + first_far[i, p]
            onward(i, p).start()

    for i in range(tiles):
        pieces_for(i)
        apply(i)
        finalize(i, diagonal)
        for p in range(2):
            far(i, p).start()
        if i > 0:
            combine(i - 1)
        for p in range(2):
            finalize(i, flip(bits[p][0]))
            mine(i, p).start()
        finalize(i, chan)
    combine(tiles - 1)
    total = zero
    for i in range(tiles):
        for p in range(2):
            mine(i, p).wait_recv()
            onward(i, p).wait_recv()
            value = image[rows_at(i), cols_at(chan, p)] + first_own[i, p] + second[i, p]
            parts[rows_at(i), pl.ds(p * span, span)] = value
            square = value * value
            for c in range(span // LANES):
                total = total + square[:, c * LANES:(c + 1) * LANES]
    me = row * nchan + chan
    squares[pl.ds(me, 1), :] = jnp.sum(total, axis=0, keepdims=True)

    def spread(step):
        other = (me + step) % (nrows * nchan)
        return pltpu.make_async_remote_copy(
            src_ref=squares.at[pl.ds(me, 1)], dst_ref=squares.at[pl.ds(me, 1)], send_sem=square_send.at[step], recv_sem=square_recv.at[step],
            device_id=(other % nchan, other // nchan), device_id_type=MESH)

    def arrived(step):
        other = (me + nrows * nchan - step) % (nrows * nchan)
        return pltpu.make_async_remote_copy(
            src_ref=squares.at[pl.ds(other, 1)], dst_ref=squares.at[pl.ds(other, 1)], send_sem=square_send.at[step], recv_sem=square_recv.at[step],
            device_id=(other % nchan, other // nchan), device_id_type=MESH)

    for step in range(1, nrows * nchan):
        spread(step).start()

    for s in range(2):
        @pl.when(row == roots[s])
        def _(s=s):
            for copy in bulk(s):
                copy.wait_send()
            for n in range(2 * tiles):
                onward_piece(s, n).wait_send()
            couple_copy(s).wait_send()

    @pl.when(is_mid)
    def _():
        for n in range(2):
            relay(crossed(n)).wait_send()

    @pl.when(is_end)
    def _():
        for n in range(nchips):
            relay(streamed(n)).wait_send()

    @pl.when(is_end & leading)
    def _():
        for n in range(tiles):
            fine_copy(n).wait_send()

    @pl.when(is_solver)
    def _():
        for step in range(1, 2 * nchan):
            table_copy(step).wait_send()
        for n in range(1, nchips):
            amp_copy(n).wait_send()

    @pl.when(jnp.logical_not(is_solver))
    def _():
        start_copy(0, row).wait_send()

    for i in range(tiles):
        for p in range(2):
            far(i, p).wait_send()
            mine(i, p).wait_send()
            onward(i, p).wait_send()
    for step in range(1, nrows * nchan):
        arrived(step).wait_recv()
    everything = jnp.sum(jnp.sum(squares[...], axis=0, keepdims=True), axis=1, keepdims=True)
    total_out[...] = jnp.broadcast_to(everything, total_out.shape)
    for step in range(1, nrows * nchan):
        spread(step).wait_send()


def run_cycle(nchan, nrows, positions, residual, psf):
    slab, ncols = residual.shape[1:]
    shard, patch = psf.shape[1:]
    steps, chunks = positions.shape[1], patch // LANES
    nchips, tiles, cols = nrows // 2, slab // 8, ncols // nchan
    rows = slab * (nrows + 2)
    dma, f32, i32 = pltpu.SemaphoreType.DMA, jnp.float32, jnp.int32
    anywhere = pl.BlockSpec(memory_space=pl.ANY)
    vmem = pl.BlockSpec(memory_space=pltpu.VMEM)
    slots = ncols // LANES + 1 + (chunks + 1) * steps
    stage = pltpu.VMEM((tiles, 2, 8, cols // 2), f32)
    small = pltpu.VMEM((8, LANES), f32)
    return pl.pallas_call(
        functools.partial(cycle_kernel, nchan, nrows),
        out_shape=(OUT((slab, ncols), f32), OUT((slab, cols), f32), OUT((8, LANES), f32)),
        in_specs=[pl.BlockSpec(memory_space=pltpu.SMEM), anywhere, anywhere],
        out_specs=(vmem, vmem, vmem),
        scratch_shapes=[
            pltpu.VMEM((tiles, slots, 8, LANES), f32), pltpu.VMEM((rows, patch), f32), pltpu.VMEM((chunks, rows, LANES), f32),
            pltpu.VMEM((chunks, shard, LANES), f32), pltpu.VMEM((steps, 8, LANES), f32), pltpu.VMEM((steps, LANES), f32),
            pltpu.VMEM((steps, LANES), f32), small, pltpu.VMEM((nrows, 8, LANES), f32),
            pltpu.VMEM((2 * nchan, steps + 8, LANES), f32), small, pltpu.VMEM((steps, LANES), i32), pltpu.VMEM((8, LANES), i32),
            stage, stage, stage, stage, pltpu.VMEM((nrows * nchan, LANES), f32),
            pltpu.SMEM((steps, LANES), i32), pltpu.SMEM((8, LANES), i32), pltpu.SMEM((8, LANES), f32),
            pltpu.SemaphoreType.REGULAR, dma((tiles,)), dma((chunks,)), dma((3,)), dma((4 * nchips,)), dma((nchips + 1,)),
            dma((nchips + 1, 2)), dma((nchips + 1,)), dma((2 * tiles,)), dma((2 * tiles,)), dma((2 * tiles,)),
            dma, dma((nrows,)), dma, dma, dma((2 * nchan,)), dma((2 * nchan,)), dma((nchips,)), dma,
        ] + [dma((tiles, 2))] * 6 + [dma((nrows * nchan,))] * 2,
        compiler_params=pltpu.CompilerParams(collective_id=0, has_side_effects=True),
        name="minor_cycle",
    )(positions, residual, psf)


def write_kernel(count, image, parts, total, image_out, normalized, scaled, sems):
    slab, tiles = image.shape[0], image.shape[0] // 8
    copies = [pltpu.make_async_copy(image.at[pl.ds(8 * t, 8)], image_out.at[0, pl.ds(8 * t, 8)], sems.at[t]) for t in range(tiles)]
    for copy in copies:
        copy.start()
    scale = lax.rsqrt(total[0:1, 0:1] / count + 1e-06)
    for t in range(tiles):
        rows = pl.ds(8 * t, 8)
        scaled[rows, :] = parts[rows, :] * scale
        copies.append(pltpu.make_async_copy(scaled.at[rows], normalized.at[rows], sems.at[tiles + t]))
        copies[-1].start()
    for copy in copies:
        copy.wait()


def write_outputs(count, image, parts, total):
    f32 = jnp.float32
    anywhere, vmem = pl.BlockSpec(memory_space=pl.ANY), pl.BlockSpec(memory_space=pltpu.VMEM)
    return pl.pallas_call(
        functools.partial(write_kernel, count),
        out_shape=(jax.ShapeDtypeStruct((1,) + image.shape, f32), jax.ShapeDtypeStruct(parts.shape, f32)),
        in_specs=[vmem, vmem, vmem],
        out_specs=(anywhere, anywhere),
        scratch_shapes=[pltpu.VMEM(parts.shape, f32), pltpu.SemaphoreType.DMA((image.shape[0] // 4,))],
        name="write_outputs",
        compiler_params=pltpu.CompilerParams(vmem_limit_bytes=4 * 2**20),
    )(*(pltpu.with_memory_space_constraint(x, pltpu.VMEM) for x in (image, parts, total)))


def on_device(residual, psf, positions):
    nchan, nrows = lax.axis_size("chan"), lax.axis_size("rows")
    slab, ncols = residual.shape[1:]
    shard, patch = psf.shape[1:]
    steps = positions.shape[0]
    central = slab * nrows == shard and shard * nrows == patch
    powers = all(n & (n - 1) == 0 for n in (slab, shard, patch)) and patch >= LANES
    lines = nchan == 4 and nrows == 8 and slab % 16 == 0 and ncols % (16 * LANES) == 0 and ncols <= LANES * LANES
    if not (central and powers and lines and steps % 8 == 0 and steps <= LANES and patch < LANES * LANES):
        return on_any_device(residual, psf, positions)
    image, parts, total = run_cycle(nchan, nrows, positions.T, residual, psf)
    return write_outputs(slab * nrows * ncols, image, parts, total)


def on_any_device(residual, psf, positions):
    chan_id = lax.axis_index("chan")
    nchan = lax.axis_size("chan")
    row_id = lax.axis_index("rows")
    nrows = lax.axis_size("rows")
    slab = residual.shape[1]
    ncols = residual.shape[2]
    own_psf = psf[0]
    shard_rows = own_psf.shape[0]
    patch = own_psf.shape[1]
    half = patch // 2
    first = row_id * slab
    chan_hot = (jnp.arange(nchan) == chan_id).astype(jnp.float32)
    full_psf = lax.all_gather(own_psf, "rows", axis=0, tiled=True)
    padded_psf = jnp.pad(full_psf, ((slab, slab), (0, 0)))
    zero = jnp.int32(0)

    def subtract(image, row, col, amount):
        offset = first - row + half
        touches = jnp.logical_and(offset > -slab, offset < patch)
        start = jnp.clip(offset + slab, 0, patch + slab)
        psf_rows = lax.dynamic_slice(padded_psf, (start, zero), (slab, patch))
        window = lax.dynamic_slice(image, (zero, col - half), (slab, patch))
        scale = jnp.where(touches, amount, 0.0)
        return lax.dynamic_update_slice(image, window - scale * psf_rows, (zero, col - half))

    image = residual[0]
    peak_rows = positions[:, 0]
    peak_cols = positions[:, 1]
    inside = jnp.logical_and(peak_rows >= first, peak_rows < first + slab)
    local_rows = jnp.clip(peak_rows - first, 0, slab - 1)
    start_values = jnp.where(inside, image[local_rows, peak_cols], 0.0)
    row_offset = peak_rows[:, None] - peak_rows[None, :] + half - row_id * shard_rows
    col_offset = peak_cols[:, None] - peak_cols[None, :] + half
    owned = (row_offset >= 0) & (row_offset < shard_rows) & (col_offset >= 0) & (col_offset < patch)
    couple = own_psf[jnp.clip(row_offset, 0, shard_rows - 1), jnp.clip(col_offset, 0, patch - 1)]
    couple = jnp.where(owned, couple, 0.0)
    start_table, couple_table = lax.psum(
        (chan_hot[:, None] * start_values[None, :], chan_hot[:, None, None] * couple[None, :, :]),
        ("chan", "rows"),
    )

    def solve(k, amps):
        taken = jnp.sum(amps * lax.dynamic_index_in_dim(couple_table, k, 1, False), axis=1)
        value = lax.dynamic_index_in_dim(start_table, k, 1, False) - taken
        amp = 0.25 * (value + jnp.sum(value) / nchan)
        return lax.dynamic_update_index_in_dim(amps, amp, k, 1)

    amps = lax.fori_loop(0, STEPS, solve, jnp.zeros((nchan, STEPS), jnp.float32))
    own_amps = jnp.sum(chan_hot[:, None] * amps, axis=0)

    def apply(k, image):
        return subtract(image, positions[k, 0], positions[k, 1], own_amps[k])

    image = lax.fori_loop(0, STEPS, apply, image)
    count = slab * nrows * ncols
    parts = lax.psum_scatter(image, "chan", scatter_dimension=1, tiled=True)
    total = lax.psum(jnp.sum(parts * parts), ("chan", "rows"))
    normalized = parts * lax.rsqrt(total / count + 1e-06)
    return (image[None], normalized)


def solution(mesh):
    return jax.shard_map(
        on_device,
        mesh=mesh,
        in_specs=(P("chan", "rows", None), P("chan", "rows", None), P()),
        out_specs=(P("chan", "rows", None), P("rows", "chan")),
        check_vma=False,
    )
```

time: 93.2 us -> 74.8 us (0.80)
  Pallas kernels: 88.2 us -> 74 us
  other arithmetic: 1.87 us -> 0 us
  local copies, waits for them, and re-layouts: 1.19 us -> 0 us
    pallas_call x4 -> x2, Pallas kernels: 88.2 us -> 74 us  [the longest x1 72.4 us: run_cycle(): pl.pallas_call(functools.partial(cycle_kernel, nchan, nrows), out_shape=(...]
    mul x1 -> x0, other arithmetic: 1.87 us -> none  [sum_channels(): return parts * lax.rsqrt(total[0, 0] / (slab * nrows * ncols) + 1e-06)]
    slice x1 -> x0, local copies, waits for them, and re-layouts: 1.19 us -> none  [sum_channels(): return parts * lax.rsqrt(total[0, 0] / (slab * nrows * ncols) + 1e-06)]
where the time goes in v1:
time: 74.8 us; the launch traced here: 74.6 us
  Pallas kernels  74 us (99%)
    pallas_call x1, Pallas kernels, run_cycle(): pl.pallas_call(functools.partial(cycle_kernel, nchan, nrows), out_shape=(...  72.4 us
    pallas_call x1, Pallas kernels, write_outputs(): pl.pallas_call(functools.partial(write_kernel, count), out_shape=(jax.Sha...  1.55 us

profile of v1, /device:TPU:0, one launch (start us, length us, event | category | flops | bytes accessed | tf_op | source)
XLA Modules:
  0.0 74.6 jit_solution(16948903705393376496)
XLA Ops:
  0.6 72.4 %minor_cycle.1 = (f32[32,16384]{1,0:T(8,128)S(1)}, f32[32,4096]{1,0:T(8,128)S(1)}, f32[8,128]{1,0:T(8,128)S(1)}) custom-call(s32[2,32]{1,0:T(2,128)} %bitcast.1, f32[1,32,16384]{2,1,0:T(8,128)} %res.1, f32[1,256,2048]{2,1,0:T(8,128)} %psf.1), custom_call_target="tpu_custom_call" | custom-call | tf_op jit(solution)/shard_map/minor_cycle/pallas_call | solution.py:531
  73.1 1.5 %write_outputs.1 = (f32[1,32,16384]{2,1,0:T(8,128)}, f32[32,4096]{1,0:T(8,128)}) custom-call(f32[32,16384]{1,0:T(8,128)S(1)} %get-tuple-element.5.image, f32[32,4096]{1,0:T(8,128)S(1)} %get-tuple-element.6.parts, f32[8,128]{1,0:T(8,128)S(1)} %get-tuple-element.7.total), custom_call_target="tpu_custom_call" | custom-call | tf_op jit(solution)/shard_map/write_outputs/pallas_call | solution.py:570

commit v2 on v1

--- a/solution.py
+++ b/solution.py
@@ -21,7 +21,7 @@
 
 def cycle_kernel(nchan, nrows, pos, res, psf, image, parts, total_out,
                  work, land, patch_v, psf_v, grid, couple_v, couple_in, start_v, start_in, tables, amps_v, prev_v, last_v,
-                 first_far, first_own, passed, second, squares, prev_s, last_s, amps_s,
+                 first_far, first_own, passed, second, squares, changes, prev_s, last_s, amps_s,
                  ready, band_sem, psf_sem, index_sem, send_sem, unit_recv, recv_sem, relay_sem, fine_send, fine_recv, fine_relay,
                  start_send, start_recv, couple_send, couple_recv, table_send, table_recv, amp_send, amp_recv,
                  far_send, far_recv, own_send, own_recv, pass_send, pass_recv, square_send, square_recv):
@@ -102,7 +102,7 @@
 
         for u in near:
             for h in order:
-                add(u, end, h, slab, 2 * end + h, recv_sem.at[u - end, h])
+                add(u, end, h, slab, 2 * end + (s if u == near[-1] else h), recv_sem.at[u - end, h])
         for u in across:
             for h in range(2):
                 add(u, other, h, slab, 2 * other + h, recv_sem.at[u - other, h])
@@ -320,26 +320,59 @@
         begin = jnp.where(side == 0, nchips - 1, 0) * unit
         relayout(land, begin, begin, 2 * unit)
 
+    amps_copy = pltpu.make_async_copy(amps_v, amps_s, index_sem.at[2])
+    leading = core == side
+
+    def half_unit(m, h):
+        begin = pl.multiple_of(m * unit + h * slab, 8)
+        relayout(land, begin, begin, slab)
+
+    def relay_half(m, h):
+        return pltpu.make_async_remote_copy(
+            src_ref=held(m, h), dst_ref=held(m, h), send_sem=relay_sem.at[nchips + 1 + h], recv_sem=recv_sem.at[m, h],
+            device_id=(chan, partner), device_id_type=MESH)
+
     @pl.when(is_end)
     def _():
-        for n in range(nchips):
+        for n in range(nchips - 1):
             pass_on(streamed(n))
-        for n in range(nchips):
-            arrival(streamed(n), 1 - core).wait_recv()
-        begin = jnp.where(side == 0, 0, 1) * unit
-        relayout(land, begin, begin, nchips * unit)
-
-    @pl.when(jnp.logical_not(is_solver))
-    def _():
+            if n > 0:
+                arrival(streamed(n - 1), 1 - core).wait_recv()
+                for h in range(2):
+                    half_unit(streamed(n - 1), h)
         amp_copy(1).wait_recv()
-
-    amps_copy = pltpu.make_async_copy(amps_v, amps_s, index_sem.at[2])
-    amps_copy.start()
+        amps_copy.start()
+        arrival(streamed(nchips - 2), 1 - core).wait_recv()
+        for h in range(2):
+            half_unit(streamed(nchips - 2), h)
+
+    @pl.when(is_end & leading)
+    def _():
+        for n in range(2):
+            h = jnp.where(side == 0, n, 1 - n)
+            arrival(streamed(nchips - 1), h).wait_recv()
+            relay_half(streamed(nchips - 1), h).start()
+            half_unit(streamed(nchips - 1), h)
+
+    @pl.when(is_end & jnp.logical_not(leading))
+    def _():
+        for n in range(2):
+            h = jnp.where(side == 0, n, 1 - n)
+            arrival(streamed(nchips - 1), h).wait_recv()
+            half_unit(streamed(nchips - 1), h)
+
+    @pl.when(is_root)
+    def _():
+        amp_copy(1).wait_recv()
+
+    @pl.when(is_mid)
+    def _():
+        amps_copy.start()
+
     for copy in index_copies:
         copy.wait()
     amps_copy.wait()
 
-    leading = core == side
     cols = ncols // nchan
     span = cols // 2
     bits = ((1, 2), (2, 1))
@@ -378,36 +411,48 @@
     def fetch(n):
         fine_copy(n).wait_recv()
 
-    def pieces_for(i):
+    def tick(n):
         @pl.when(is_end & leading)
         def _():
-            fetch(i)
-            fine_copy(i).start()
-            relayout(land, fine_at(i), fine_at(i), 8)
-
+            fetch(n)
+            fine_copy(n).start()
+            relayout(land, fine_at(n), fine_at(n), 8)
+
+    def late(n):
         @pl.when(is_end & jnp.logical_not(leading))
         def _():
-            for n in (range(tiles + 1) if i == 0 else (tiles + i,)):
-                fetch(n)
-                relayout(land, fine_at(n), fine_at(n), 8)
-
-    def apply(i):
-        t = tile_at(i)
-        lift = top + 8 * t
-
-        def two(kk, carry):
-            for k in (2 * kk, 2 * kk + 1):
+            fetch(n)
+            relayout(land, fine_at(n), fine_at(n), 8)
+
+    def scale_and_shift(i):
+        lift = top + 8 * tile_at(i)
+
+        def four(g, carry):
+            for n in range(4):
+                k = 4 * g + n
                 amp = amps_s[chan, k]
                 begin = lift - pos[0, k]
                 shift = (pos[1, k] - half) & (LANES - 1)
                 keep = lane8 < shift
                 moved = [zero] + [pltpu.roll(patch_v[c, pl.ds(begin, 8), :] * amp, shift, 1) for c in range(chunks)] + [zero]
                 for m in range(width):
-                    change = jnp.where(keep, moved[m], moved[m + 1])
-                    work[t, base + width * k + m] = work[t, prev_s[k, m]] - change
+                    changes[width * k + m] = jnp.where(keep, moved[m], moved[m + 1])
             return carry
 
-        lax.fori_loop(0, steps // 2, two, 0)
+        lax.fori_loop(0, steps // 4, four, 0)
+
+    def subtract(i):
+        t = tile_at(i)
+
+        def four(g, carry):
+            for n in range(4):
+                k = 4 * g + n
+                after = [work[t, prev_s[k, m]] - changes[width * k + m] for m in range(width)]
+                for m in range(width):
+                    work[t, base + width * k + m] = after[m]
+            return carry
+
+        lax.fori_loop(0, steps // 4, four, 0)
 
     def finalize(i, c):
         rows = rows_at(i)
@@ -428,18 +473,35 @@
             onward(i, p).start()
 
     for i in range(tiles):
-        pieces_for(i)
-        apply(i)
+        if i == 0:
+            tick(0)
+            for n in range(tiles):
+                late(n)
+        late(tiles + i)
+        scale_and_shift(i)
+        if i == 0:
+            tick(1)
+        subtract(i)
         finalize(i, diagonal)
         for p in range(2):
             far(i, p).start()
+        if i == 0:
+            for n in range(2, tiles):
+                tick(n)
+        for p in range(2):
+            finalize(i, flip(bits[p][0]))
+        finalize(i, chan)
+        if i == tiles - 1:
+            for p in range(2):
+                mine(i - 1, p).start()
         if i > 0:
             combine(i - 1)
-        for p in range(2):
-            finalize(i, flip(bits[p][0]))
-            mine(i, p).start()
-        finalize(i, chan)
+        if i < tiles - 2:
+            for p in range(2):
+                mine(i, p).start()
     combine(tiles - 1)
+    for p in range(2):
+        mine(tiles - 1, p).start()
     total = zero
     for i in range(tiles):
         for p in range(2):
@@ -484,11 +546,13 @@
 
     @pl.when(is_end)
     def _():
-        for n in range(nchips):
+        for n in range(nchips - 1):
             relay(streamed(n)).wait_send()
 
     @pl.when(is_end & leading)
     def _():
+        for h in range(2):
+            relay_half(streamed(nchips - 1), h).wait_send()
         for n in range(tiles):
             fine_copy(n).wait_send()
 
@@ -538,10 +602,10 @@
             pltpu.VMEM((chunks, shard, LANES), f32), pltpu.VMEM((steps, 8, LANES), f32), pltpu.VMEM((steps, LANES), f32),
             pltpu.VMEM((steps, LANES), f32), small, pltpu.VMEM((nrows, 8, LANES), f32),
             pltpu.VMEM((2 * nchan, steps + 8, LANES), f32), small, pltpu.VMEM((steps, LANES), i32), pltpu.VMEM((8, LANES), i32),
-            stage, stage, stage, stage, pltpu.VMEM((nrows * nchan, LANES), f32),
+            stage, stage, stage, stage, pltpu.VMEM((nrows * nchan, LANES), f32), pltpu.VMEM(((chunks + 1) * steps, 8, LANES), f32),
             pltpu.SMEM((steps, LANES), i32), pltpu.SMEM((8, LANES), i32), pltpu.SMEM((8, LANES), f32),
             pltpu.SemaphoreType.REGULAR, dma((tiles,)), dma((chunks,)), dma((3,)), dma((4 * nchips,)), dma((nchips + 1,)),
-            dma((nchips + 1, 2)), dma((nchips + 1,)), dma((2 * tiles,)), dma((2 * tiles,)), dma((2 * tiles,)),
+            dma((nchips + 1, 2)), dma((nchips + 3,)), dma((2 * tiles,)), dma((2 * tiles,)), dma((2 * tiles,)),
             dma, dma((nrows,)), dma, dma, dma((2 * nchan,)), dma((2 * nchan,)), dma((nchips,)), dma,
         ] + [dma((tiles, 2))] * 6 + [dma((nrows * nchan,))] * 2,
         compiler_params=pltpu.CompilerParams(collective_id=0, has_side_effects=True),

time: 74.8 us -> 63.7 us (0.85)
  Pallas kernels: 74 us -> 62.9 us
    pallas_call x1, Pallas kernels: 72.4 us -> 61.4 us  [run_cycle(): pl.pallas_call(functools.partial(cycle_kernel, nchan, nrows), out_shape=(...]
where the time goes in v2:
time: 63.7 us; the launch traced here: 63.6 us
  Pallas kernels  62.9 us (99%)
  between operations  0.64 us (1%)
    pallas_call x1, Pallas kernels, run_cycle(): pl.pallas_call(functools.partial(cycle_kernel, nchan, nrows), out_shape=(...  61.4 us
    pallas_call x1, Pallas kernels, write_outputs(): pl.pallas_call(functools.partial(write_kernel, count), out_shape=(jax.Sha...  1.55 us

profile of v2, /device:TPU:0, one launch (start us, length us, event | category | flops | bytes accessed | tf_op | source)
XLA Modules:
  0.0 63.6 jit_solution(12617757944372916610)
XLA Ops:
  0.6 61.4 %minor_cycle.1 = (f32[32,16384]{1,0:T(8,128)S(1)}, f32[32,4096]{1,0:T(8,128)S(1)}, f32[8,128]{1,0:T(8,128)S(1)}) custom-call(s32[2,32]{1,0:T(2,128)} %bitcast.1, f32[1,32,16384]{2,1,0:T(8,128)} %res.1, f32[1,256,2048]{2,1,0:T(8,128)} %psf.1), custom_call_target="tpu_custom_call" | custom-call | tf_op jit(solution)/shard_map/minor_cycle/pallas_call | solution.py:595
  62.0 1.5 %write_outputs.1 = (f32[1,32,16384]{2,1,0:T(8,128)}, f32[32,4096]{1,0:T(8,128)}) custom-call(f32[32,16384]{1,0:T(8,128)S(1)} %get-tuple-element.5.image, f32[32,4096]{1,0:T(8,128)S(1)} %get-tuple-element.6.parts, f32[8,128]{1,0:T(8,128)S(1)} %get-tuple-element.7.total), custom_call_target="tpu_custom_call" | custom-call | tf_op jit(solution)/shard_map/write_outputs/pallas_call | solution.py:634

commit v3 on v2

--- a/solution.py
+++ b/solution.py
@@ -21,10 +21,10 @@
 
 def cycle_kernel(nchan, nrows, pos, res, psf, image, parts, total_out,
                  work, land, patch_v, psf_v, grid, couple_v, couple_in, start_v, start_in, tables, amps_v, prev_v, last_v,
-                 first_far, first_own, passed, second, squares, changes, prev_s, last_s, amps_s,
+                 first_far, first_own, passed, second, squares, changes, pair_v, sum_v, prev_s, last_s, amps_s, pair_s,
                  ready, band_sem, psf_sem, index_sem, send_sem, unit_recv, recv_sem, relay_sem, fine_send, fine_recv, fine_relay,
                  start_send, start_recv, couple_send, couple_recv, table_send, table_recv, amp_send, amp_recv,
-                 far_send, far_recv, own_send, own_recv, pass_send, pass_recv, square_send, square_recv):
+                 far_send, far_recv, own_send, own_recv, pass_send, pass_recv, square_send, square_recv, guest_sem):
     chan, row = lax.axis_index("chan"), lax.axis_index("rows")
     chip, core = row // 2, row % 2
     partner = row + 1 - 2 * core
@@ -36,6 +36,8 @@
     unit, tiles, blocks = 2 * slab, slab // 8, ncols // LANES
     base, width = blocks + 1, chunks + 1
     first = row * slab
+    begins_at = [z - (1 if z == (nchips - 1) // 2 else 0) for z in range(nchips)]
+    lead = jnp.where(chip == (nchips - 1) // 2, 1, 0)
     roots = (nchips - 1, nchips)
     solvers = (roots[0] ^ 1, roots[1] ^ 1)
     is_root = jnp.logical_or(row == roots[0], row == roots[1])
@@ -80,6 +82,25 @@
         last = jnp.where((inside >= 0) & (inside < width), inside + (base + width * k), last)
     prev_v[...] = prev
     last_v[...] = last
+    lane32 = lax.broadcasted_iota(jnp.int32, (steps, LANES), 1)
+    rows_from = jnp.zeros((steps, LANES), jnp.int32)
+    cols_from = jnp.zeros((steps, LANES), jnp.int32)
+    for k in range(steps):
+        rows_from = rows_from + jnp.where(krow == k, pos[0, k], 0) - jnp.where(lane32 == k, pos[0, k], 0)
+        cols_from = cols_from + jnp.where(krow == k, pos[1, k], 0) - jnp.where(lane32 == k, pos[1, k], 0)
+    rows_from = rows_from + half - row * shard
+    cols_from = cols_from + half
+    owned = (rows_from >= 0) & (rows_from < shard) & (cols_from >= 0) & (cols_from < patch) & (lane32 < krow)
+    pair_v[0] = (cols_from >> 7) & (chunks - 1)
+    pair_v[1] = ((rows_from >> 3) << 3) & (shard - 1)
+    pair_v[2] = (lane32 - cols_from) & (LANES - 1)
+    pair_v[3] = jnp.where(owned, (rows_from & 7) * LANES + lane32, -1)
+    pair_copy = pltpu.make_async_copy(pair_v, pair_s, index_sem.at[3])
+
+    @pl.when(is_root)
+    def _():
+        pair_copy.start()
+
     index_copies = [pltpu.make_async_copy(prev_v, prev_s, index_sem.at[0]), pltpu.make_async_copy(last_v, last_s, index_sem.at[1])]
     for copy in index_copies:
         copy.start()
@@ -92,22 +113,22 @@
         order = (0, 1) if s == 0 else (1, 0)
         near = list(range(nchips)) if s == 0 else list(range(2 * nchips - 1, nchips - 1, -1))
         across = [nchips - 1 - n if s == 0 else nchips + n for n in range(nchips // 2)]
-        local = [u for u in range(mid, mid + nchips + 1) if (u < nchips) == (s == 0)]
+        local = range(s * nchips, (s + 1) * nchips)
         out = []
 
         def add(u, z, h, rows, to_row, sem):
             out.append(pltpu.make_async_remote_copy(
-                src_ref=psf.at[0, pl.ds((u % nchips) * unit + h * slab, rows)], dst_ref=land.at[pl.ds((u - z) * unit + h * slab, rows)],
+                src_ref=psf.at[0, pl.ds((u % nchips) * unit + h * slab, rows)], dst_ref=land.at[pl.ds((u - begins_at[z]) * unit + h * slab, rows)],
                 send_sem=send_sem.at[len(out)], recv_sem=sem, device_id=(chan, to_row), device_id_type=MESH))
 
         for u in near:
             for h in order:
-                add(u, end, h, slab, 2 * end + (s if u == near[-1] else h), recv_sem.at[u - end, h])
+                add(u, end, h, slab, 2 * end + (s if u == near[-1] else h), recv_sem.at[u - begins_at[end], h])
         for u in across:
             for h in range(2):
-                add(u, other, h, slab, 2 * other + h, recv_sem.at[u - other, h])
+                add(u, other, h, slab, 2 * other + h, recv_sem.at[u - begins_at[other], h])
         for u in local:
-            add(u, mid, 0, unit, solvers[s], unit_recv.at[u - mid])
+            add(u, mid, 0, unit, solvers[s], unit_recv.at[u - begins_at[mid]])
         return out
 
     for s in range(2):
@@ -115,6 +136,26 @@
         def _(s=s):
             for copy in bulk(s):
                 copy.start()
+
+    helper = row + 2 - 4 * side
+    helped = row - 2 + 4 * side
+
+    def tile_at(i):
+        return jnp.where(side == 0, i, tiles - 1 - i)
+
+    def tile_rows(t):
+        return pl.ds(pl.multiple_of(8 * t, 8), 8)
+
+    lent = pltpu.make_async_remote_copy(
+        src_ref=res.at[0, tile_rows(tile_at(tiles - 1))], dst_ref=image.at[pl.ds(slab, 8)], send_sem=guest_sem.at[0], recv_sem=guest_sem.at[1],
+        device_id=(chan, helper), device_id_type=MESH)
+    given = pltpu.make_async_remote_copy(
+        src_ref=parts.at[pl.ds(slab, 8)], dst_ref=parts.at[tile_rows(tile_at(tiles - 1))], send_sem=guest_sem.at[2], recv_sem=guest_sem.at[3],
+        device_id=(chan, helped), device_id_type=MESH)
+
+    @pl.when(is_end)
+    def _():
+        lent.start()
 
     for step in range(1, nchan):
         pl.semaphore_signal(ready, inc=1, device_id=((chan + step) % nchan, row), device_id_type=MESH)
@@ -154,21 +195,14 @@
     def _():
         for copy in loads:
             copy.wait()
-        low = row * shard - half
+        pair_copy.wait()
 
         def fill(k, carry):
-            rk, qk = pos[0, k] - low, pos[1, k] + half
-
-            def test(g, acc):
-                for i in range(8):
-                    j = g * 8 + i
-                    r, c = rk - pos[0, j], qk - pos[1, j]
-                    owned = (r >= 0) & (r < shard) & (c >= 0) & (c < patch) & (j < k)
-                    tile = psf_v[(c >> 7) & (chunks - 1), pl.ds(((r >> 3) << 3) & (shard - 1), 8), :]
-                    acc = pick(tile, r, c, j, owned, number, acc)
-                return acc
-
-            grid[k] = lax.fori_loop(0, (k + 7) >> 3, test, zero)
+            acc = zero
+            for j in range(steps):
+                tile = psf_v[pair_s[0, k, j], pl.ds(pair_s[1, k, j], 8), :]
+                acc = jnp.where(number == pair_s[3, k, j], pltpu.roll(tile, pair_s[2, k, j], 1), acc)
+            grid[k] = acc
             return carry
 
         lax.fori_loop(0, steps, fill, 0)
@@ -197,7 +231,7 @@
         relay(m).start()
 
     def crossed(n):
-        return jnp.where(side == 0, nchips - 1 + n, 1 - n)
+        return jnp.where(side == 0, nchips + n, 1 - n)
 
     def streamed(n):
         return jnp.where(side == 0, n, nchips - n)
@@ -286,7 +320,7 @@
         u = nchips - s
         j = n if s == 0 else 2 * tiles - 1 - n
         return pltpu.make_async_remote_copy(
-            src_ref=land.at[pl.ds((u - mid) * unit + 8 * j, 8)], dst_ref=land.at[pl.ds((u - end) * unit + 8 * j, 8)],
+            src_ref=land.at[pl.ds((u - begins_at[mid]) * unit + 8 * j, 8)], dst_ref=land.at[pl.ds((u - begins_at[end]) * unit + 8 * j, 8)],
             send_sem=fine_send.at[n], recv_sem=fine_recv.at[n], device_id=(chan, 2 * end + j // tiles), device_id_type=MESH)
 
     def fine_copy(n):
@@ -295,29 +329,28 @@
             send_sem=fine_relay.at[n], recv_sem=fine_recv.at[n], device_id=(chan, partner), device_id_type=MESH)
 
     for s in range(2):
-        mid = (nchips - 1 + s) // 2
-        local = [u for u in range(mid, mid + nchips + 1) if (u < nchips) == (s == 0)]
+        offset = s * nchips - begins_at[(nchips - 1 + s) // 2]
 
         @pl.when(row == roots[s])
-        def _(s=s, mid=mid, local=local):
+        def _(s=s, offset=offset):
             arrival(crossed(0), 1 - core).wait_recv()
             for n in range(2 * tiles):
                 onward_piece(s, n).start()
-            relayout(psf_v, (local[0] % nchips) * unit, (local[0] - mid) * unit, len(local) * unit)
+            relayout(psf_v, 0, offset * unit, nchips * unit)
 
         @pl.when(row == solvers[s])
-        def _(s=s, mid=mid, local=local):
+        def _(s=s, offset=offset):
             arrival(crossed(0), 1 - core).wait_recv()
-            for u in local:
+            for u in range(nchips):
                 pltpu.make_async_remote_copy(
-                    src_ref=held(u - mid, 0, unit), dst_ref=held(u - mid, 0, unit), send_sem=send_sem.at[0], recv_sem=unit_recv.at[u - mid],
+                    src_ref=held(u + offset, 0, unit), dst_ref=held(u + offset, 0, unit), send_sem=send_sem.at[0], recv_sem=unit_recv.at[u + offset],
                     device_id=(chan, partner), device_id_type=MESH).wait_recv()
-            relayout(land, (local[0] - mid) * unit, (local[0] - mid) * unit, len(local) * unit)
+            relayout(land, offset * unit, offset * unit, nchips * unit)
 
     @pl.when(is_mid)
     def _():
         arrival(crossed(1), 1 - core).wait_recv()
-        begin = jnp.where(side == 0, nchips - 1, 0) * unit
+        begin = jnp.where(side == 0, nchips, 0) * unit
         relayout(land, begin, begin, 2 * unit)
 
     amps_copy = pltpu.make_async_copy(amps_v, amps_s, index_sem.at[2])
@@ -329,7 +362,7 @@
 
     def relay_half(m, h):
         return pltpu.make_async_remote_copy(
-            src_ref=held(m, h), dst_ref=held(m, h), send_sem=relay_sem.at[nchips + 1 + h], recv_sem=recv_sem.at[m, h],
+            src_ref=held(m, h), dst_ref=held(m, h), send_sem=relay_sem.at[nchips + 2 + h], recv_sem=recv_sem.at[m, h],
             device_id=(chan, partner), device_id_type=MESH)
 
     @pl.when(is_end)
@@ -376,7 +409,6 @@
     cols = ncols // nchan
     span = cols // 2
     bits = ((1, 2), (2, 1))
-    top = core * slab + slab * nrows
 
     def flip(bit):
         if bit == 1:
@@ -385,11 +417,20 @@
 
     diagonal = 3 - chan
 
-    def tile_at(i):
-        return jnp.where(side == 0, i, tiles - 1 - i)
-
-    def rows_at(i):
-        return pl.ds(pl.multiple_of(8 * tile_at(i), 8), 8)
+    def tile_of(n):
+        if n == 0:
+            return tile_at(0)
+        return jnp.where(is_mid, tiles if n == 1 else tile_at(n - 1), tile_at(n))
+
+    def rows_at(n):
+        return tile_rows(tile_of(n))
+
+    def lift_of(n):
+        own_lift = slab * nrows + lead * unit + core * slab + 8 * tile_of(n)
+        if n != 1:
+            return own_lift
+        guest_lift = slab * nrows + side * unit + core * slab + 8 * tile_at(tiles - 1)
+        return jnp.where(is_mid, guest_lift, own_lift)
 
     def cols_at(c, p):
         return pl.ds(pl.multiple_of(c * cols + p * span, LANES), span)
@@ -425,11 +466,11 @@
             relayout(land, fine_at(n), fine_at(n), 8)
 
     def scale_and_shift(i):
-        lift = top + 8 * tile_at(i)
-
-        def four(g, carry):
-            for n in range(4):
-                k = 4 * g + n
+        lift = lift_of(i)
+
+        def eight(g, carry):
+            for n in range(8):
+                k = 8 * g + n
                 amp = amps_s[chan, k]
                 begin = lift - pos[0, k]
                 shift = (pos[1, k] - half) & (LANES - 1)
@@ -439,20 +480,20 @@
                     changes[width * k + m] = jnp.where(keep, moved[m], moved[m + 1])
             return carry
 
-        lax.fori_loop(0, steps // 4, four, 0)
+        lax.fori_loop(0, steps // 8, eight, 0)
 
     def subtract(i):
-        t = tile_at(i)
-
-        def four(g, carry):
-            for n in range(4):
-                k = 4 * g + n
+        t = tile_of(i)
+
+        def eight(g, carry):
+            for n in range(8):
+                k = 8 * g + n
                 after = [work[t, prev_s[k, m]] - changes[width * k + m] for m in range(width)]
                 for m in range(width):
                     work[t, base + width * k + m] = after[m]
             return carry
 
-        lax.fori_loop(0, steps // 4, four, 0)
+        lax.fori_loop(0, steps // 8, eight, 0)
 
     def finalize(i, c):
         rows = rows_at(i)
@@ -461,7 +502,7 @@
         def body(g, carry):
             for n in range(8):
                 b = c * per + g * 8 + n
-                image[rows, block_at(b)] = work[tile_at(i), last_s[0, b]]
+                image[rows, block_at(b)] = work[tile_of(i), last_s[0, b]]
             return carry
 
         lax.fori_loop(0, per // 8, body, 0)
@@ -472,46 +513,114 @@
             passed[i, p] = image[rows_at(i), cols_at(flip(bits[p][1]), p)] + first_far[i, p]
             onward(i, p).start()
 
-    for i in range(tiles):
-        if i == 0:
-            tick(0)
-            for n in range(tiles):
-                late(n)
-        late(tiles + i)
-        scale_and_shift(i)
-        if i == 0:
-            tick(1)
-        subtract(i)
-        finalize(i, diagonal)
+    def own(n):
         for p in range(2):
-            far(i, p).start()
-        if i == 0:
-            for n in range(2, tiles):
-                tick(n)
-        for p in range(2):
-            finalize(i, flip(bits[p][0]))
-        finalize(i, chan)
-        if i == tiles - 1:
-            for p in range(2):
-                mine(i - 1, p).start()
-        if i > 0:
-            combine(i - 1)
-        if i < tiles - 2:
-            for p in range(2):
-                mine(i, p).start()
-    combine(tiles - 1)
-    for p in range(2):
-        mine(tiles - 1, p).start()
-    total = zero
-    for i in range(tiles):
-        for p in range(2):
-            mine(i, p).wait_recv()
-            onward(i, p).wait_recv()
-            value = image[rows_at(i), cols_at(chan, p)] + first_own[i, p] + second[i, p]
-            parts[rows_at(i), pl.ds(p * span, span)] = value
+            mine(n, p).wait_recv()
+            onward(n, p).wait_recv()
+            value = image[rows_at(n), cols_at(chan, p)] + first_own[n, p] + second[n, p]
+            parts[rows_at(n), pl.ds(p * span, span)] = value
             square = value * value
+            total = zero
             for c in range(span // LANES):
                 total = total + square[:, c * LANES:(c + 1) * LANES]
+            sum_v[...] = sum_v[...] + total
+
+    def start_far(n):
+        for p in range(2):
+            far(n, p).start()
+
+    def start_mine(n):
+        for p in range(2):
+            mine(n, p).start()
+
+    def finish(n):
+        for p in range(2):
+            finalize(n, flip(bits[p][0]))
+        finalize(n, chan)
+
+    sum_v[...] = zero
+    for n in range(tiles - 1):
+        if n == 0:
+            tick(0)
+            for piece in range(tiles):
+                late(piece)
+        if n == 1:
+            @pl.when(is_mid)
+            def _():
+                lent.wait_recv()
+
+                def guest(b, carry):
+                    work[tiles, b] = image[pl.ds(slab, 8), block_at(b)]
+                    return carry
+
+                lax.fori_loop(0, blocks, guest, 0, unroll=4)
+
+        late(tiles + n)
+        scale_and_shift(n)
+        if n == 0:
+            tick(1)
+        subtract(n)
+        finalize(n, diagonal)
+        start_far(n)
+        if n == 0:
+            for piece in range(2, tiles):
+                tick(piece)
+        finish(n)
+        if n > 0:
+            combine(n - 1)
+        if n < tiles - 2:
+            start_mine(n)
+
+    @pl.when(is_mid)
+    def _():
+        start_mine(tiles - 2)
+
+    late(2 * tiles - 1)
+    scale_and_shift(tiles - 1)
+
+    @pl.when(is_end)
+    def _():
+        combine(tiles - 2)
+        start_mine(tiles - 2)
+
+    subtract(tiles - 1)
+    finalize(tiles - 1, diagonal)
+
+    @pl.when(is_mid)
+    def _():
+        start_far(tiles - 1)
+
+    finish(tiles - 1)
+
+    @pl.when(is_mid)
+    def _():
+        combine(tiles - 2)
+        own(1)
+        given.start()
+        scale_and_shift(tiles)
+        subtract(tiles)
+        finalize(tiles, diagonal)
+        start_far(tiles)
+        finish(tiles)
+        start_mine(tiles - 1)
+        combine(tiles - 1)
+        combine(tiles)
+        start_mine(tiles)
+
+    own(0)
+
+    @pl.when(is_end)
+    def _():
+        own(1)
+
+    own(2)
+
+    @pl.when(is_mid)
+    def _():
+        own(tiles - 1)
+        own(tiles)
+
+    total = sum_v[...]
     me = row * nchan + chan
     squares[pl.ds(me, 1), :] = jnp.sum(total, axis=0, keepdims=True)
 
@@ -567,11 +676,26 @@
     def _():
         start_copy(0, row).wait_send()
 
-    for i in range(tiles):
+    def sent(n):
         for p in range(2):
-            far(i, p).wait_send()
-            mine(i, p).wait_send()
-            onward(i, p).wait_send()
+            far(n, p).wait_send()
+            mine(n, p).wait_send()
+            onward(n, p).wait_send()
+
+    for n in range(tiles - 1):
+        sent(n)
+
+    @pl.when(is_mid)
+    def _():
+        sent(tiles - 1)
+        sent(tiles)
+        given.wait_send()
+
+    @pl.when(is_end)
+    def _():
+        lent.wait_send()
+        given.wait_recv()
+
     for step in range(1, nrows * nchan):
         arrived(step).wait_recv()
     everything = jnp.sum(jnp.sum(squares[...], axis=0, keepdims=True), axis=1, keepdims=True)
@@ -585,36 +709,36 @@
     shard, patch = psf.shape[1:]
     steps, chunks = positions.shape[1], patch // LANES
     nchips, tiles, cols = nrows // 2, slab // 8, ncols // nchan
-    rows = slab * (nrows + 2)
+    rows = slab * (nrows + 4)
     dma, f32, i32 = pltpu.SemaphoreType.DMA, jnp.float32, jnp.int32
     anywhere = pl.BlockSpec(memory_space=pl.ANY)
     vmem = pl.BlockSpec(memory_space=pltpu.VMEM)
     slots = ncols // LANES + 1 + (chunks + 1) * steps
-    stage = pltpu.VMEM((tiles, 2, 8, cols // 2), f32)
+    stage = pltpu.VMEM((tiles + 1, 2, 8, cols // 2), f32)
     small = pltpu.VMEM((8, LANES), f32)
     return pl.pallas_call(
         functools.partial(cycle_kernel, nchan, nrows),
-        out_shape=(OUT((slab, ncols), f32), OUT((slab, cols), f32), OUT((8, LANES), f32)),
+        out_shape=(OUT((slab + 8, ncols), f32), OUT((slab + 8, cols), f32), OUT((8, LANES), f32)),
         in_specs=[pl.BlockSpec(memory_space=pltpu.SMEM), anywhere, anywhere],
         out_specs=(vmem, vmem, vmem),
         scratch_shapes=[
-            pltpu.VMEM((tiles, slots, 8, LANES), f32), pltpu.VMEM((rows, patch), f32), pltpu.VMEM((chunks, rows, LANES), f32),
+            pltpu.VMEM((tiles + 1, slots, 8, LANES), f32), pltpu.VMEM((rows, patch), f32), pltpu.VMEM((chunks, rows, LANES), f32),
             pltpu.VMEM((chunks, shard, LANES), f32), pltpu.VMEM((steps, 8, LANES), f32), pltpu.VMEM((steps, LANES), f32),
             pltpu.VMEM((steps, LANES), f32), small, pltpu.VMEM((nrows, 8, LANES), f32),
             pltpu.VMEM((2 * nchan, steps + 8, LANES), f32), small, pltpu.VMEM((steps, LANES), i32), pltpu.VMEM((8, LANES), i32),
-            stage, stage, stage, stage, pltpu.VMEM((nrows * nchan, LANES), f32), pltpu.VMEM(((chunks + 1) * steps, 8, LANES), f32),
-            pltpu.SMEM((steps, LANES), i32), pltpu.SMEM((8, LANES), i32), pltpu.SMEM((8, LANES), f32),
-            pltpu.SemaphoreType.REGULAR, dma((tiles,)), dma((chunks,)), dma((3,)), dma((4 * nchips,)), dma((nchips + 1,)),
-            dma((nchips + 1, 2)), dma((nchips + 3,)), dma((2 * tiles,)), dma((2 * tiles,)), dma((2 * tiles,)),
+            stage, stage, stage, stage, pltpu.VMEM((nrows * nchan, LANES), f32), pltpu.VMEM(((chunks + 1) * steps, 8, LANES), f32), pltpu.VMEM((4, steps, LANES), i32), small,
+            pltpu.SMEM((steps, LANES), i32), pltpu.SMEM((8, LANES), i32), pltpu.SMEM((8, LANES), f32), pltpu.SMEM((4, steps, LANES), i32),
+            pltpu.SemaphoreType.REGULAR, dma((tiles,)), dma((chunks,)), dma((4,)), dma((4 * nchips,)), dma((nchips + 2,)),
+            dma((nchips + 2, 2)), dma((nchips + 4,)), dma((2 * tiles,)), dma((2 * tiles,)), dma((2 * tiles,)),
             dma, dma((nrows,)), dma, dma, dma((2 * nchan,)), dma((2 * nchan,)), dma((nchips,)), dma,
-        ] + [dma((tiles, 2))] * 6 + [dma((nrows * nchan,))] * 2,
+        ] + [dma((tiles + 1, 2))] * 6 + [dma((nrows * nchan,))] * 2 + [dma((4,))],
         compiler_params=pltpu.CompilerParams(collective_id=0, has_side_effects=True),
         name="minor_cycle",
     )(positions, residual, psf)
 
 
 def write_kernel(count, image, parts, total, image_out, normalized, scaled, sems):
-    slab, tiles = image.shape[0], image.shape[0] // 8
+    slab, tiles = scaled.shape[0], scaled.shape[0] // 8
     copies = [pltpu.make_async_copy(image.at[pl.ds(8 * t, 8)], image_out.at[0, pl.ds(8 * t, 8)], sems.at[t]) for t in range(tiles)]
     for copy in copies:
         copy.start()
@@ -628,15 +752,15 @@
         copy.wait()
 
 
-def write_outputs(count, image, parts, total):
-    f32 = jnp.float32
+def write_outputs(count, slab, image, parts, total):
+    f32, ncols, cols = jnp.float32, image.shape[1], parts.shape[1]
     anywhere, vmem = pl.BlockSpec(memory_space=pl.ANY), pl.BlockSpec(memory_space=pltpu.VMEM)
     return pl.pallas_call(
         functools.partial(write_kernel, count),
-        out_shape=(jax.ShapeDtypeStruct((1,) + image.shape, f32), jax.ShapeDtypeStruct(parts.shape, f32)),
+        out_shape=(jax.ShapeDtypeStruct((1, slab, ncols), f32), jax.ShapeDtypeStruct((slab, cols), f32)),
         in_specs=[vmem, vmem, vmem],
         out_specs=(anywhere, anywhere),
-        scratch_shapes=[pltpu.VMEM(parts.shape, f32), pltpu.SemaphoreType.DMA((image.shape[0] // 4,))],
+        scratch_shapes=[pltpu.VMEM((slab, cols), f32), pltpu.SemaphoreType.DMA((slab // 4,))],
         name="write_outputs",
         compiler_params=pltpu.CompilerParams(vmem_limit_bytes=4 * 2**20),
     )(*(pltpu.with_memory_space_constraint(x, pltpu.VMEM) for x in (image, parts, total)))
@@ -653,7 +777,7 @@
     if not (central and powers and lines and steps % 8 == 0 and steps <= LANES and patch < LANES * LANES):
         return on_any_device(residual, psf, positions)
     image, parts, total = run_cycle(nchan, nrows, positions.T, residual, psf)
-    return write_outputs(slab * nrows * ncols, image, parts, total)
+    return write_outputs(slab * nrows * ncols, slab, image, parts, total)
 
 
 def on_any_device(residual, psf, positions):

time: 63.7 us -> 61.6 us (0.967)
  Pallas kernels: 62.9 us -> 60.8 us
    pallas_call x1, Pallas kernels: 61.4 us -> 59.2 us  [run_cycle(): pl.pallas_call(functools.partial(cycle_kernel, nchan, nrows), out_shape=(...]
where the time goes in v3:
time: 61.6 us; the launch traced here: 61.4 us
  Pallas kernels  60.8 us (99%)
  between operations  0.64 us (1%)
    pallas_call x1, Pallas kernels, run_cycle(): pl.pallas_call(functools.partial(cycle_kernel, nchan, nrows), out_shape=(...  59.2 us
    pallas_call x1, Pallas kernels, write_outputs(): pl.pallas_call(functools.partial(write_kernel, count), out_shape=(jax.Sha...  1.55 us

profile of v3, /device:TPU:0, one launch (start us, length us, event | category | flops | bytes accessed | tf_op | source)
XLA Modules:
  0.0 61.4 jit_solution(9208209586285406528)
XLA Ops:
  0.6 59.2 %minor_cycle.1 = (f32[40,16384]{1,0:T(8,128)S(1)}, f32[40,4096]{1,0:T(8,128)S(1)}, f32[8,128]{1,0:T(8,128)S(1)}) custom-call(s32[2,32]{1,0:T(2,128)} %bitcast.1, f32[1,32,16384]{2,1,0:T(8,128)} %res.1, f32[1,256,2048]{2,1,0:T(8,128)} %psf.1), custom_call_target="tpu_custom_call" | custom-call | tf_op jit(solution)/shard_map/minor_cycle/pallas_call | solution.py:719
  59.9 1.5 %write_outputs.1 = (f32[1,32,16384]{2,1,0:T(8,128)}, f32[32,4096]{1,0:T(8,128)}) custom-call(f32[40,16384]{1,0:T(8,128)S(1)} %get-tuple-element.5.image, f32[40,4096]{1,0:T(8,128)S(1)} %get-tuple-element.6.parts, f32[8,128]{1,0:T(8,128)S(1)} %get-tuple-element.7.total), custom_call_target="tpu_custom_call" | custom-call | tf_op jit(solution)/shard_map/write_outputs/pallas_call | solution.py:758

commit v4 on v3

--- a/solution.py
+++ b/solution.py
@@ -55,7 +55,7 @@
     bands = [pltpu.make_async_copy(res.at[0, pl.ds(8 * t, 8)], image.at[pl.ds(8 * t, 8)], band_sem.at[t]) for t in range(tiles)]
     for copy in bands:
         copy.start()
-    loads = [pltpu.make_async_copy(psf.at[0, :, pl.ds(c * LANES, LANES)], psf_v.at[c], psf_sem.at[c]) for c in range(chunks)]
+    loads = [pltpu.make_async_copy(psf.at[0, :, pl.ds(c * LANES, LANES)], psf_v.at[pl.ds(c * shard, shard)], psf_sem.at[c]) for c in range(chunks)]
 
     barrier = pltpu.get_barrier_semaphore()
     for step in range(1, nrows):
@@ -91,10 +91,9 @@
     rows_from = rows_from + half - row * shard
     cols_from = cols_from + half
     owned = (rows_from >= 0) & (rows_from < shard) & (cols_from >= 0) & (cols_from < patch) & (lane32 < krow)
-    pair_v[0] = (cols_from >> 7) & (chunks - 1)
-    pair_v[1] = ((rows_from >> 3) << 3) & (shard - 1)
-    pair_v[2] = (lane32 - cols_from) & (LANES - 1)
-    pair_v[3] = jnp.where(owned, (rows_from & 7) * LANES + lane32, -1)
+    pair_v[0] = ((cols_from >> 7) & (chunks - 1)) * shard + (((rows_from >> 3) << 3) & (shard - 1))
+    pair_v[1] = (lane32 - cols_from) & (LANES - 1)
+    pair_v[2] = jnp.where(owned, (rows_from & 7) * LANES + lane32, -1)
     pair_copy = pltpu.make_async_copy(pair_v, pair_s, index_sem.at[3])
 
     @pl.when(is_root)
@@ -137,8 +136,9 @@
             for copy in bulk(s):
                 copy.start()
 
-    helper = row + 2 - 4 * side
-    helped = row - 2 + 4 * side
+    trail = 1 - side
+    is_lead, is_trail = is_end & (core == side), is_end & (core == trail)
+    host = jnp.where(core == side, 0, 1)
 
     def tile_at(i):
         return jnp.where(side == 0, i, tiles - 1 - i)
@@ -146,16 +146,15 @@
     def tile_rows(t):
         return pl.ds(pl.multiple_of(8 * t, 8), 8)
 
-    lent = pltpu.make_async_remote_copy(
-        src_ref=res.at[0, tile_rows(tile_at(tiles - 1))], dst_ref=image.at[pl.ds(slab, 8)], send_sem=guest_sem.at[0], recv_sem=guest_sem.at[1],
-        device_id=(chan, helper), device_id_type=MESH)
-    given = pltpu.make_async_remote_copy(
-        src_ref=parts.at[pl.ds(slab, 8)], dst_ref=parts.at[tile_rows(tile_at(tiles - 1))], send_sem=guest_sem.at[2], recv_sem=guest_sem.at[3],
-        device_id=(chan, helped), device_id_type=MESH)
-
-    @pl.when(is_end)
-    def _():
-        lent.start()
+    def lent(g):
+        return pltpu.make_async_remote_copy(
+            src_ref=res.at[0, tile_rows(tile_at(tiles - 2 + g))], dst_ref=image.at[pl.ds(slab, 8)], send_sem=guest_sem.at[g], recv_sem=guest_sem.at[2],
+            device_id=(chan, nchips - 2 + 2 * side + (side if g == 0 else trail)), device_id_type=MESH)
+
+    def given(g):
+        return pltpu.make_async_remote_copy(
+            src_ref=parts.at[pl.ds(slab, 8)], dst_ref=parts.at[tile_rows(tile_at(tiles - 2 + g))], send_sem=guest_sem.at[3], recv_sem=guest_sem.at[4 + g],
+            device_id=(chan, side * (nrows - 2) + trail), device_id_type=MESH)
 
     for step in range(1, nchan):
         pl.semaphore_signal(ready, inc=1, device_id=((chan + step) % nchan, row), device_id_type=MESH)
@@ -191,21 +190,27 @@
         def _(s=s):
             start_copy(s, row).start()
 
+    @pl.when(is_trail)
+    def _():
+        for g in range(2):
+            lent(g).start()
+
     @pl.when(is_root)
     def _():
         for copy in loads:
             copy.wait()
         pair_copy.wait()
 
-        def fill(k, carry):
+        def fill(count, k, carry):
             acc = zero
-            for j in range(steps):
-                tile = psf_v[pair_s[0, k, j], pl.ds(pair_s[1, k, j], 8), :]
-                acc = jnp.where(number == pair_s[3, k, j], pltpu.roll(tile, pair_s[2, k, j], 1), acc)
+            for j in range(count):
+                tile = psf_v[pl.ds(pair_s[0, k, j], 8), :]
+                acc = jnp.where(number == pair_s[2, k, j], pltpu.roll(tile, pair_s[1, k, j], 1), acc)
             grid[k] = acc
             return carry
 
-        lax.fori_loop(0, steps, fill, 0)
+        for g in range(steps // 8):
+            lax.fori_loop(8 * g, 8 * g + 8, functools.partial(fill, 8 * g + 8), 0)
         couple_v[...] = jnp.sum(grid[...], axis=1)
 
     for s in range(2):
@@ -240,13 +245,14 @@
         def body(g, carry):
             take, put = pl.multiple_of(source_row + 8 * g, 8), pl.multiple_of(dest_row + 8 * g, 8)
             for c in range(chunks):
-                tile = source[c, pl.ds(take, 8), :] if len(source.shape) == 3 else source[pl.ds(take, 8), pl.ds(c * LANES, LANES)]
+                narrow = source.shape[1] == LANES
+                tile = source[pl.ds(pl.multiple_of(c * shard + take, 8), 8), :] if narrow else source[pl.ds(take, 8), pl.ds(c * LANES, LANES)]
                 patch_v[c, pl.ds(put, 8), :] = tile
             return carry
 
         lax.fori_loop(0, rows // 8, body, 0)
 
-    @pl.when(is_mid)
+    @pl.when(is_root)
     def _():
         pass_on(crossed(0))
 
@@ -278,8 +284,9 @@
             tables[me_table, pl.ds(steps, 8), :] = jnp.broadcast_to(jnp.sum(total, axis=0, keepdims=True), total.shape)
             for step in range(1, 2 * nchan):
                 table_copy(step).start()
-
-    @pl.when(is_mid)
+            pass_on(crossed(0))
+
+    @pl.when(is_root)
     def _():
         pass_on(crossed(1))
 
@@ -303,11 +310,12 @@
             amp = 0.25 * (value + jnp.sum(value, axis=0, keepdims=True) / nchan)
             return jnp.where(lane == k, amp, amps)
 
-        amps = lax.fori_loop(0, steps, solve, jnp.zeros((nchan, LANES), jnp.float32))
+        amps = lax.fori_loop(0, steps, solve, jnp.zeros((nchan, LANES), jnp.float32), unroll=4)
         amps_v[pl.ds(0, nchan), :] = amps
         amps_v[pl.ds(nchan, 8 - nchan), :] = jnp.zeros((8 - nchan, LANES), jnp.float32)
         for n in range(1, nchips):
             amp_copy(n).start()
+        pass_on(crossed(1))
 
     def fine_piece(n):
         return jnp.where(side == 0, n, 2 * tiles - 1 - n)
@@ -429,7 +437,7 @@
         own_lift = slab * nrows + lead * unit + core * slab + 8 * tile_of(n)
         if n != 1:
             return own_lift
-        guest_lift = slab * nrows + side * unit + core * slab + 8 * tile_at(tiles - 1)
+        guest_lift = slab * nrows + side * unit + trail * slab + 8 * tile_at(tiles - 2 + host)
         return jnp.where(is_mid, guest_lift, own_lift)
 
     def cols_at(c, p):
@@ -539,15 +547,15 @@
         finalize(n, chan)
 
     sum_v[...] = zero
-    for n in range(tiles - 1):
+    for n in range(2):
         if n == 0:
             tick(0)
             for piece in range(tiles):
                 late(piece)
-        if n == 1:
+        else:
             @pl.when(is_mid)
             def _():
-                lent.wait_recv()
+                lent(0).wait_recv()
 
                 def guest(b, carry):
                     work[tiles, b] = image[pl.ds(slab, 8), block_at(b)]
@@ -566,59 +574,86 @@
             for piece in range(2, tiles):
                 tick(piece)
         finish(n)
-        if n > 0:
-            combine(n - 1)
-        if n < tiles - 2:
-            start_mine(n)
+        if n == 0:
+            start_mine(0)
+    combine(0)
+
+    @pl.when(jnp.logical_not(is_trail))
+    def _():
+        start_mine(1)
+
+    late(tiles + 2)
+    scale_and_shift(2)
+
+    @pl.when(is_trail)
+    def _():
+        combine(1)
+        start_mine(1)
+
+    subtract(2)
+    finalize(2, diagonal)
+
+    @pl.when(jnp.logical_not(is_trail))
+    def _():
+        start_far(2)
+
+    finish(2)
+
+    @pl.when(jnp.logical_not(is_trail))
+    def _():
+        combine(1)
 
     @pl.when(is_mid)
     def _():
-        start_mine(tiles - 2)
-
-    late(2 * tiles - 1)
-    scale_and_shift(tiles - 1)
+        start_mine(2)
+
+    late(tiles + 3)
+    scale_and_shift(3)
+    subtract(3)
+    finalize(3, diagonal)
+
+    @pl.when(jnp.logical_not(is_trail))
+    def _():
+        start_far(3)
+
+    finish(3)
+
+    @pl.when(is_lead)
+    def _():
+        start_mine(2)
+        combine(2)
+        combine(3)
+        start_mine(3)
+
+    @pl.when(is_mid)
+    def _():
+        combine(2)
+        own(1)
+        given(host).start()
+        scale_and_shift(4)
+        subtract(4)
+        finalize(4, diagonal)
+        start_far(4)
+        finish(4)
+        start_mine(3)
+        combine(3)
+        combine(4)
+        start_mine(4)
+
+    own(0)
 
     @pl.when(is_end)
     def _():
-        combine(tiles - 2)
-        start_mine(tiles - 2)
-
-    subtract(tiles - 1)
-    finalize(tiles - 1, diagonal)
+        own(1)
+
+    @pl.when(jnp.logical_not(is_trail))
+    def _():
+        own(2)
+        own(3)
 
     @pl.when(is_mid)
     def _():
-        start_far(tiles - 1)
-
-    finish(tiles - 1)
-
-    @pl.when(is_mid)
-    def _():
-        combine(tiles - 2)
-        own(1)
-        given.start()
-        scale_and_shift(tiles)
-        subtract(tiles)
-        finalize(tiles, diagonal)
-        start_far(tiles)
-        finish(tiles)
-        start_mine(tiles - 1)
-        combine(tiles - 1)
-        combine(tiles)
-        start_mine(tiles)
-
-    own(0)
-
-    @pl.when(is_end)
-    def _():
-        own(1)
-
-    own(2)
-
-    @pl.when(is_mid)
-    def _():
-        own(tiles - 1)
-        own(tiles)
+        own(4)
 
     total = sum_v[...]
     me = row * nchan + chan
@@ -682,19 +717,24 @@
             mine(n, p).wait_send()
             onward(n, p).wait_send()
 
-    for n in range(tiles - 1):
+    for n in range(2):
         sent(n)
 
+    @pl.when(jnp.logical_not(is_trail))
+    def _():
+        sent(2)
+        sent(3)
+
     @pl.when(is_mid)
     def _():
-        sent(tiles - 1)
-        sent(tiles)
-        given.wait_send()
-
-    @pl.when(is_end)
-    def _():
-        lent.wait_send()
-        given.wait_recv()
+        sent(4)
+        given(host).wait_send()
+
+    @pl.when(is_trail)
+    def _():
+        for g in range(2):
+            lent(g).wait_send()
+            given(g).wait_recv()
 
     for step in range(1, nrows * nchan):
         arrived(step).wait_recv()
@@ -723,15 +763,15 @@
         out_specs=(vmem, vmem, vmem),
         scratch_shapes=[
             pltpu.VMEM((tiles + 1, slots, 8, LANES), f32), pltpu.VMEM((rows, patch), f32), pltpu.VMEM((chunks, rows, LANES), f32),
-            pltpu.VMEM((chunks, shard, LANES), f32), pltpu.VMEM((steps, 8, LANES), f32), pltpu.VMEM((steps, LANES), f32),
+            pltpu.VMEM((chunks * shard, LANES), f32), pltpu.VMEM((steps, 8, LANES), f32), pltpu.VMEM((steps, LANES), f32),
             pltpu.VMEM((steps, LANES), f32), small, pltpu.VMEM((nrows, 8, LANES), f32),
             pltpu.VMEM((2 * nchan, steps + 8, LANES), f32), small, pltpu.VMEM((steps, LANES), i32), pltpu.VMEM((8, LANES), i32),
-            stage, stage, stage, stage, pltpu.VMEM((nrows * nchan, LANES), f32), pltpu.VMEM(((chunks + 1) * steps, 8, LANES), f32), pltpu.VMEM((4, steps, LANES), i32), small,
-            pltpu.SMEM((steps, LANES), i32), pltpu.SMEM((8, LANES), i32), pltpu.SMEM((8, LANES), f32), pltpu.SMEM((4, steps, LANES), i32),
+            stage, stage, stage, stage, pltpu.VMEM((nrows * nchan, LANES), f32), pltpu.VMEM(((chunks + 1) * steps, 8, LANES), f32), pltpu.VMEM((3, steps, LANES), i32), small,
+            pltpu.SMEM((steps, LANES), i32), pltpu.SMEM((8, LANES), i32), pltpu.SMEM((8, LANES), f32), pltpu.SMEM((3, steps, LANES), i32),
             pltpu.SemaphoreType.REGULAR, dma((tiles,)), dma((chunks,)), dma((4,)), dma((4 * nchips,)), dma((nchips + 2,)),
             dma((nchips + 2, 2)), dma((nchips + 4,)), dma((2 * tiles,)), dma((2 * tiles,)), dma((2 * tiles,)),
             dma, dma((nrows,)), dma, dma, dma((2 * nchan,)), dma((2 * nchan,)), dma((nchips,)), dma,
-        ] + [dma((tiles + 1, 2))] * 6 + [dma((nrows * nchan,))] * 2 + [dma((4,))],
+        ] + [dma((tiles + 1, 2))] * 6 + [dma((nrows * nchan,))] * 2 + [dma((6,))],
         compiler_params=pltpu.CompilerParams(collective_id=0, has_side_effects=True),
         name="minor_cycle",
     )(positions, residual, psf)
@@ -773,7 +813,7 @@
     steps = positions.shape[0]
     central = slab * nrows == shard and shard * nrows == patch
     powers = all(n & (n - 1) == 0 for n in (slab, shard, patch)) and patch >= LANES
-    lines = nchan == 4 and nrows == 8 and slab % 16 == 0 and ncols % (16 * LANES) == 0 and ncols <= LANES * LANES
+    lines = nchan == 4 and nrows == 8 and slab == 32 and ncols % (16 * LANES) == 0 and ncols <= LANES * LANES
     if not (central and powers and lines and steps % 8 == 0 and steps <= LANES and patch < LANES * LANES):
         return on_any_device(residual, psf, positions)
     image, parts, total = run_cycle(nchan, nrows, positions.T, residual, psf)

time: 61.6 us -> 58.9 us (0.956)
  Pallas kernels: 60.8 us -> 58 us
    pallas_call x1, Pallas kernels: 59.2 us -> 56.5 us  [run_cycle(): pl.pallas_call(functools.partial(cycle_kernel, nchan, nrows), out_shape=(...]
where the time goes in v4:
time: 58.9 us; the launch traced here: 58.7 us
  Pallas kernels  58 us (98%)
  between operations  0.64 us (1%)
    pallas_call x1, Pallas kernels, run_cycle(): pl.pallas_call(functools.partial(cycle_kernel, nchan, nrows), out_shape=(...  56.5 us
    pallas_call x1, Pallas kernels, write_outputs(): pl.pallas_call(functools.partial(write_kernel, count), out_shape=(jax.Sha...  1.55 us

profile of v4, /device:TPU:0, one launch (start us, length us, event | category | flops | bytes accessed | tf_op | source)
XLA Modules:
  0.0 58.7 jit_solution(4389663550430477172)
XLA Ops:
  0.6 56.5 %minor_cycle.1 = (f32[40,16384]{1,0:T(8,128)S(1)}, f32[40,4096]{1,0:T(8,128)S(1)}, f32[8,128]{1,0:T(8,128)S(1)}) custom-call(s32[2,32]{1,0:T(2,128)} %bitcast.1, f32[1,32,16384]{2,1,0:T(8,128)} %res.1, f32[1,256,2048]{2,1,0:T(8,128)} %psf.1), custom_call_target="tpu_custom_call" | custom-call | tf_op jit(solution)/shard_map/minor_cycle/pallas_call | solution.py:759
  57.1 1.5 %write_outputs.1 = (f32[1,32,16384]{2,1,0:T(8,128)}, f32[32,4096]{1,0:T(8,128)}) custom-call(f32[40,16384]{1,0:T(8,128)S(1)} %get-tuple-element.5.image, f32[40,4096]{1,0:T(8,128)S(1)} %get-tuple-element.6.parts, f32[8,128]{1,0:T(8,128)S(1)} %get-tuple-element.7.total), custom_call_target="tpu_custom_call" | custom-call | tf_op jit(solution)/shard_map/write_outputs/pallas_call | solution.py:798

commit v5 on v4

--- a/solution.py
+++ b/solution.py
@@ -11,6 +11,7 @@
 LANES = 128
 MESH = pl.DeviceIdType.MESH
 OUT = pltpu.VMEM
+VMEM = 67043328
 
 
 def pick(tile, row, col, lane_to, owned, number, acc):
@@ -136,9 +137,11 @@
             for copy in bulk(s):
                 copy.start()
 
-    trail = 1 - side
-    is_lead, is_trail = is_end & (core == side), is_end & (core == trail)
-    host = jnp.where(core == side, 0, 1)
+    early = core == side
+    is_lead, is_trail = is_end & early, is_end & jnp.logical_not(early)
+    doubled = is_mid & jnp.logical_not(early)
+    sends = jnp.where(is_end, jnp.where(early, tiles - 1, tiles - 2), jnp.where(early, tiles + 1, tiles + 2))
+    count = jnp.where(is_end, tiles, sends)
 
     def tile_at(i):
         return jnp.where(side == 0, i, tiles - 1 - i)
@@ -146,15 +149,18 @@
     def tile_rows(t):
         return pl.ds(pl.multiple_of(8 * t, 8), 8)
 
+    def guest_tile(g):
+        return tile_at(jnp.where(early, tiles - 1, tiles - 2 + g))
+
     def lent(g):
         return pltpu.make_async_remote_copy(
-            src_ref=res.at[0, tile_rows(tile_at(tiles - 2 + g))], dst_ref=image.at[pl.ds(slab, 8)], send_sem=guest_sem.at[g], recv_sem=guest_sem.at[2],
-            device_id=(chan, nchips - 2 + 2 * side + (side if g == 0 else trail)), device_id_type=MESH)
+            src_ref=res.at[0, tile_rows(guest_tile(g))], dst_ref=image.at[tile_rows(tiles + g)], send_sem=guest_sem.at[g], recv_sem=guest_sem.at[2 + g],
+            device_id=(chan, row + 2 - 4 * side), device_id_type=MESH)
 
     def given(g):
         return pltpu.make_async_remote_copy(
-            src_ref=parts.at[pl.ds(slab, 8)], dst_ref=parts.at[tile_rows(tile_at(tiles - 2 + g))], send_sem=guest_sem.at[3], recv_sem=guest_sem.at[4 + g],
-            device_id=(chan, side * (nrows - 2) + trail), device_id_type=MESH)
+            src_ref=parts.at[tile_rows(tiles + g)], dst_ref=parts.at[tile_rows(guest_tile(g))], send_sem=guest_sem.at[4 + g], recv_sem=guest_sem.at[6 + g],
+            device_id=(chan, row - 2 + 4 * side), device_id_type=MESH)
 
     for step in range(1, nchan):
         pl.semaphore_signal(ready, inc=1, device_id=((chan + step) % nchan, row), device_id_type=MESH)
@@ -190,10 +196,13 @@
         def _(s=s):
             start_copy(s, row).start()
 
+    @pl.when(is_end)
+    def _():
+        lent(0).start()
+
     @pl.when(is_trail)
     def _():
-        for g in range(2):
-            lent(g).start()
+        lent(1).start()
 
     @pl.when(is_root)
     def _():
@@ -286,10 +295,6 @@
                 table_copy(step).start()
             pass_on(crossed(0))
 
-    @pl.when(is_root)
-    def _():
-        pass_on(crossed(1))
-
     def amp_copy(n):
         return pltpu.make_async_remote_copy(
             src_ref=amps_v, dst_ref=amps_v, send_sem=amp_send.at[n], recv_sem=amp_recv,
@@ -315,7 +320,6 @@
         amps_v[pl.ds(nchan, 8 - nchan), :] = jnp.zeros((8 - nchan, LANES), jnp.float32)
         for n in range(1, nchips):
             amp_copy(n).start()
-        pass_on(crossed(1))
 
     def fine_piece(n):
         return jnp.where(side == 0, n, 2 * tiles - 1 - n)
@@ -355,14 +359,16 @@
                     device_id=(chan, partner), device_id_type=MESH).wait_recv()
             relayout(land, offset * unit, offset * unit, nchips * unit)
 
+    def relayout_crossed(n):
+        begin = pl.multiple_of(crossed(n) * unit, 8)
+        relayout(land, begin, begin, unit)
+
     @pl.when(is_mid)
     def _():
-        arrival(crossed(1), 1 - core).wait_recv()
-        begin = jnp.where(side == 0, nchips, 0) * unit
-        relayout(land, begin, begin, 2 * unit)
+        relayout_crossed(0)
 
     amps_copy = pltpu.make_async_copy(amps_v, amps_s, index_sem.at[2])
-    leading = core == side
+    leading = early
 
     def half_unit(m, h):
         begin = pl.multiple_of(m * unit + h * slab, 8)
@@ -425,20 +431,22 @@
 
     diagonal = 3 - chan
 
+    def is_guest(n):
+        return (n == 0) | (doubled & (n == 2))
+
+    def own_index(n):
+        return jnp.where(is_mid, n - 1 - jnp.where(doubled & (n > 2), 1, 0), n)
+
     def tile_of(n):
-        if n == 0:
-            return tile_at(0)
-        return jnp.where(is_mid, tiles if n == 1 else tile_at(n - 1), tile_at(n))
+        return jnp.where(is_mid & is_guest(n), tiles + n // 2, tile_at(own_index(n)))
 
     def rows_at(n):
         return tile_rows(tile_of(n))
 
     def lift_of(n):
-        own_lift = slab * nrows + lead * unit + core * slab + 8 * tile_of(n)
-        if n != 1:
-            return own_lift
-        guest_lift = slab * nrows + side * unit + trail * slab + 8 * tile_at(tiles - 2 + host)
-        return jnp.where(is_mid, guest_lift, own_lift)
+        own_lift = lead * unit + 8 * tile_at(own_index(n))
+        guest_lift = side * unit + 8 * guest_tile(n // 2)
+        return slab * nrows + core * slab + jnp.where(is_mid & is_guest(n), guest_lift, own_lift)
 
     def cols_at(c, p):
         return pl.ds(pl.multiple_of(c * cols + p * span, LANES), span)
@@ -547,114 +555,104 @@
         finalize(n, chan)
 
     sum_v[...] = zero
-    for n in range(2):
-        if n == 0:
+
+    def advance(n, carry):
+        active = n < count
+
+        @pl.when(n == 0)
+        def _():
             tick(0)
             for piece in range(tiles):
                 late(piece)
-        else:
-            @pl.when(is_mid)
-            def _():
-                lent(0).wait_recv()
-
-                def guest(b, carry):
-                    work[tiles, b] = image[pl.ds(slab, 8), block_at(b)]
-                    return carry
-
-                lax.fori_loop(0, blocks, guest, 0, unroll=4)
-
-        late(tiles + n)
-        scale_and_shift(n)
-        if n == 0:
+
+        @pl.when(is_trail & active)
+        def _():
+            late(tiles + n)
+
+        @pl.when(is_mid & is_guest(n))
+        def _():
+            lent(n // 2).wait_recv()
+
+            def guest(b, carry):
+                work[tiles + n // 2, b] = image[tile_rows(tiles + n // 2), block_at(b)]
+                return carry
+
+            lax.fori_loop(0, blocks, guest, 0, unroll=4)
+
+        @pl.when(is_mid & (n == 1))
+        def _():
+            arrival(crossed(1), 1 - core).wait_recv()
+            relayout_crossed(1)
+
+        @pl.when(active)
+        def _():
+            scale_and_shift(n)
+
+        @pl.when(n == 0)
+        def _():
             tick(1)
-        subtract(n)
-        finalize(n, diagonal)
-        start_far(n)
-        if n == 0:
+
+        @pl.when(is_mid & (n == 0))
+        def _():
+            pass_on(crossed(1))
+
+        @pl.when(n == sends)
+        def _():
+            combine(n - 1)
+            start_mine(n - 1)
+
+        @pl.when(active)
+        def _():
+            subtract(n)
+            finalize(n, diagonal)
+
+        @pl.when(n < sends)
+        def _():
+            start_far(n)
+
+        @pl.when(n == 0)
+        def _():
             for piece in range(2, tiles):
                 tick(piece)
-        finish(n)
-        if n == 0:
-            start_mine(0)
-    combine(0)
-
-    @pl.when(jnp.logical_not(is_trail))
-    def _():
-        start_mine(1)
-
-    late(tiles + 2)
-    scale_and_shift(2)
-
-    @pl.when(is_trail)
-    def _():
-        combine(1)
-        start_mine(1)
-
-    subtract(2)
-    finalize(2, diagonal)
-
-    @pl.when(jnp.logical_not(is_trail))
-    def _():
-        start_far(2)
-
-    finish(2)
-
-    @pl.when(jnp.logical_not(is_trail))
-    def _():
-        combine(1)
-
-    @pl.when(is_mid)
-    def _():
-        start_mine(2)
-
-    late(tiles + 3)
-    scale_and_shift(3)
-    subtract(3)
-    finalize(3, diagonal)
-
-    @pl.when(jnp.logical_not(is_trail))
-    def _():
-        start_far(3)
-
-    finish(3)
-
-    @pl.when(is_lead)
-    def _():
-        start_mine(2)
-        combine(2)
-        combine(3)
-        start_mine(3)
-
-    @pl.when(is_mid)
-    def _():
-        combine(2)
-        own(1)
-        given(host).start()
-        scale_and_shift(4)
-        subtract(4)
-        finalize(4, diagonal)
-        start_far(4)
-        finish(4)
-        start_mine(3)
-        combine(3)
-        combine(4)
-        start_mine(4)
-
-    own(0)
-
-    @pl.when(is_end)
-    def _():
-        own(1)
-
-    @pl.when(jnp.logical_not(is_trail))
-    def _():
-        own(2)
-        own(3)
-
-    @pl.when(is_mid)
-    def _():
-        own(4)
-
+
+        @pl.when(active)
+        def _():
+            finish(n)
+
+        @pl.when((n == sends - 1) & (n > 1))
+        def _():
+            start_mine(n - 1)
+
+        @pl.when((n > 0) & (n < sends))
+        def _():
+            combine(n - 1)
+
+        @pl.when((n == 0) | (n < sends - 2))
+        def _():
+            start_mine(n)
+
+        @pl.when(is_mid & (n == 3))
+        def _():
+            own(0)
+            given(0).start()
+
+        @pl.when(doubled & (n == 5))
+        def _():
+            own(2)
+            given(1).start()
+
+        return carry
+
+    lax.fori_loop(0, tiles + 3, advance, 0)
+
+    def settle(n, carry):
+        @pl.when((n < sends) & jnp.logical_not(is_mid & is_guest(n)))
+        def _():
+            own(n)
+
+        return carry
+
+    lax.fori_loop(0, tiles + 2, settle, 0)
     total = sum_v[...]
     me = row * nchan + chan
     squares[pl.ds(me, 1), :] = jnp.sum(total, axis=0, keepdims=True)
@@ -711,30 +709,35 @@
     def _():
         start_copy(0, row).wait_send()
 
-    def sent(n):
-        for p in range(2):
-            far(n, p).wait_send()
-            mine(n, p).wait_send()
-            onward(n, p).wait_send()
-
-    for n in range(2):
-        sent(n)
-
-    @pl.when(jnp.logical_not(is_trail))
-    def _():
-        sent(2)
-        sent(3)
+    def sent(n, carry):
+        @pl.when(n < sends)
+        def _():
+            for p in range(2):
+                far(n, p).wait_send()
+                mine(n, p).wait_send()
+                onward(n, p).wait_send()
+
+        return carry
+
+    lax.fori_loop(0, tiles + 2, sent, 0)
 
     @pl.when(is_mid)
     def _():
-        sent(4)
-        given(host).wait_send()
+        given(0).wait_send()
+
+    @pl.when(doubled)
+    def _():
+        given(1).wait_send()
+
+    @pl.when(is_end)
+    def _():
+        lent(0).wait_send()
+        given(0).wait_recv()
 
     @pl.when(is_trail)
     def _():
-        for g in range(2):
-            lent(g).wait_send()
-            given(g).wait_recv()
+        lent(1).wait_send()
+        given(1).wait_recv()
 
     for step in range(1, nrows * nchan):
         arrived(step).wait_recv()
@@ -754,15 +757,15 @@
     anywhere = pl.BlockSpec(memory_space=pl.ANY)
     vmem = pl.BlockSpec(memory_space=pltpu.VMEM)
     slots = ncols // LANES + 1 + (chunks + 1) * steps
-    stage = pltpu.VMEM((tiles + 1, 2, 8, cols // 2), f32)
+    stage = pltpu.VMEM((tiles + 2, 2, 8, cols // 2), f32)
     small = pltpu.VMEM((8, LANES), f32)
     return pl.pallas_call(
         functools.partial(cycle_kernel, nchan, nrows),
-        out_shape=(OUT((slab + 8, ncols), f32), OUT((slab + 8, cols), f32), OUT((8, LANES), f32)),
+        out_shape=(OUT((slab + 16, ncols), f32), OUT((slab + 16, cols), f32), OUT((8, LANES), f32)),
         in_specs=[pl.BlockSpec(memory_space=pltpu.SMEM), anywhere, anywhere],
         out_specs=(vmem, vmem, vmem),
         scratch_shapes=[
-            pltpu.VMEM((tiles + 1, slots, 8, LANES), f32), pltpu.VMEM((rows, patch), f32), pltpu.VMEM((chunks, rows, LANES), f32),
+            pltpu.VMEM((tiles + 2, slots, 8, LANES), f32), pltpu.VMEM((rows, patch), f32), pltpu.VMEM((chunks, rows, LANES), f32),
             pltpu.VMEM((chunks * shard, LANES), f32), pltpu.VMEM((steps, 8, LANES), f32), pltpu.VMEM((steps, LANES), f32),
             pltpu.VMEM((steps, LANES), f32), small, pltpu.VMEM((nrows, 8, LANES), f32),
             pltpu.VMEM((2 * nchan, steps + 8, LANES), f32), small, pltpu.VMEM((steps, LANES), i32), pltpu.VMEM((8, LANES), i32),
@@ -771,8 +774,8 @@
             pltpu.SemaphoreType.REGULAR, dma((tiles,)), dma((chunks,)), dma((4,)), dma((4 * nchips,)), dma((nchips + 2,)),
             dma((nchips + 2, 2)), dma((nchips + 4,)), dma((2 * tiles,)), dma((2 * tiles,)), dma((2 * tiles,)),
             dma, dma((nrows,)), dma, dma, dma((2 * nchan,)), dma((2 * nchan,)), dma((nchips,)), dma,
-        ] + [dma((tiles + 1, 2))] * 6 + [dma((nrows * nchan,))] * 2 + [dma((6,))],
-        compiler_params=pltpu.CompilerParams(collective_id=0, has_side_effects=True),
+        ] + [dma((tiles + 2, 2))] * 6 + [dma((nrows * nchan,))] * 2 + [dma((8,))],
+        compiler_params=pltpu.CompilerParams(collective_id=0, has_side_effects=True, vmem_limit_bytes=VMEM - 4 * ((slab + 16) * (ncols + cols) + 8 * LANES)),
         name="minor_cycle",
     )(positions, residual, psf)
 

time: 58.9 us -> 57.7 us (0.980)
  Pallas kernels: 58 us -> 56.9 us
    pallas_call x1, Pallas kernels: 56.5 us -> 55.4 us  [run_cycle(): pl.pallas_call(functools.partial(cycle_kernel, nchan, nrows), out_shape=(...]
where the time goes in v5:
time: 57.7 us; the launch traced here: 57.5 us
  Pallas kernels  56.9 us (99%)
  between operations  0.64 us (1%)
    pallas_call x1, Pallas kernels, run_cycle(): pl.pallas_call(functools.partial(cycle_kernel, nchan, nrows), out_shape=(...  55.4 us
    pallas_call x1, Pallas kernels, write_outputs(): pl.pallas_call(functools.partial(write_kernel, count), out_shape=(jax.Sha...  1.55 us

profile of v5, /device:TPU:0, one launch (start us, length us, event | category | flops | bytes accessed | tf_op | source)
XLA Modules:
  0.0 57.5 jit_solution(2028067788674504855)
XLA Ops:
  0.6 55.4 %minor_cycle.1 = (f32[48,16384]{1,0:T(8,128)S(1)}, f32[48,4096]{1,0:T(8,128)S(1)}, f32[8,128]{1,0:T(8,128)S(1)}) custom-call(s32[2,32]{1,0:T(2,128)} %bitcast.1, f32[1,32,16384]{2,1,0:T(8,128)} %res.1, f32[1,256,2048]{2,1,0:T(8,128)} %psf.1), custom_call_target="tpu_custom_call" | custom-call | tf_op jit(solution)/shard_map/minor_cycle/pallas_call | solution.py:762
  56.0 1.5 %write_outputs.1 = (f32[1,32,16384]{2,1,0:T(8,128)}, f32[32,4096]{1,0:T(8,128)}) custom-call(f32[48,16384]{1,0:T(8,128)S(1)} %get-tuple-element.5.image, f32[48,4096]{1,0:T(8,128)S(1)} %get-tuple-element.6.parts, f32[8,128]{1,0:T(8,128)S(1)} %get-tuple-element.7.total), custom_call_target="tpu_custom_call" | custom-call | tf_op jit(solution)/shard_map/write_outputs/pallas_call | solution.py:801

commit v6 on v5

--- a/solution.py
+++ b/solution.py
@@ -53,16 +53,30 @@
     def block_at(index):
         return pl.ds(pl.multiple_of(index * LANES, LANES), LANES)
 
+    def flip(bit):
+        if bit == 1:
+            return chan + 1 - 2 * (chan % 2)
+        return (chan + 2) % 4
+
+    barrier = pltpu.get_barrier_semaphore()
+    for bit in (1, 2):
+        pl.semaphore_signal(barrier, inc=1, device_id=(flip(bit), row), device_id_type=MESH)
+    pl.semaphore_signal(barrier, inc=1, device_id=(chan, partner), device_id_type=MESH)
+
+    @pl.when(chip > 0)
+    def _():
+        for c in range(2):
+            pl.semaphore_signal(barrier, inc=1, device_id=(chan, 2 * chip - 2 + c), device_id_type=MESH)
+
+    @pl.when(chip < nchips - 1)
+    def _():
+        for c in range(2):
+            pl.semaphore_signal(barrier, inc=1, device_id=(chan, 2 * chip + 2 + c), device_id_type=MESH)
+
     bands = [pltpu.make_async_copy(res.at[0, pl.ds(8 * t, 8)], image.at[pl.ds(8 * t, 8)], band_sem.at[t]) for t in range(tiles)]
     for copy in bands:
         copy.start()
     loads = [pltpu.make_async_copy(psf.at[0, :, pl.ds(c * LANES, LANES)], psf_v.at[pl.ds(c * shard, shard)], psf_sem.at[c]) for c in range(chunks)]
-
-    barrier = pltpu.get_barrier_semaphore()
-    for step in range(1, nrows):
-        pl.semaphore_signal(barrier, inc=1, device_id=(chan, (row + step) % nrows), device_id_type=MESH)
-    for step in range(1, nchan):
-        pl.semaphore_signal(barrier, inc=1, device_id=((chan + step) % nchan, row), device_id_type=MESH)
 
     @pl.when(is_root)
     def _():
@@ -106,7 +120,15 @@
         copy.start()
     for t in range(tiles):
         work[t, blocks] = zero
-    pl.semaphore_wait(barrier, nrows + nchan - 2)
+
+    @pl.when(is_end)
+    def _():
+        pl.semaphore_wait(barrier, 5)
+
+    @pl.when(is_mid)
+    def _():
+        pl.semaphore_wait(barrier, 7)
+
 
     def bulk(s):
         mid, end, other = (nchips - 1 + s) // 2, (nchips - 1) * s, nchips // 2 - s
@@ -162,8 +184,8 @@
             src_ref=parts.at[tile_rows(tiles + g)], dst_ref=parts.at[tile_rows(guest_tile(g))], send_sem=guest_sem.at[4 + g], recv_sem=guest_sem.at[6 + g],
             device_id=(chan, row - 2 + 4 * side), device_id_type=MESH)
 
-    for step in range(1, nchan):
-        pl.semaphore_signal(ready, inc=1, device_id=((chan + step) % nchan, row), device_id_type=MESH)
+    for bit in (1, 2):
+        pl.semaphore_signal(ready.at[0], inc=1, device_id=(flip(bit), row), device_id_type=MESH)
 
     for copy in bands:
         copy.wait()
@@ -265,7 +287,10 @@
     def _():
         pass_on(crossed(0))
 
-    pl.semaphore_wait(ready, nchan - 1)
+    pl.semaphore_wait(ready.at[0], 2)
+    for bit in (1, 2):
+        pl.semaphore_signal(ready.at[1], inc=1, device_id=(flip(bit), row), device_id_type=MESH)
+    pl.semaphore_wait(ready.at[1], 2)
     me_table = 2 * chan + side
 
     def table_copy(step):
@@ -333,7 +358,7 @@
         j = n if s == 0 else 2 * tiles - 1 - n
         return pltpu.make_async_remote_copy(
             src_ref=land.at[pl.ds((u - begins_at[mid]) * unit + 8 * j, 8)], dst_ref=land.at[pl.ds((u - begins_at[end]) * unit + 8 * j, 8)],
-            send_sem=fine_send.at[n], recv_sem=fine_recv.at[n], device_id=(chan, 2 * end + j // tiles), device_id_type=MESH)
+            send_sem=fine_send.at[n], recv_sem=fine_recv.at[n], device_id=(chan, 2 * end + (s if n == 0 else 1 - s)), device_id_type=MESH)
 
     def fine_copy(n):
         return pltpu.make_async_remote_copy(
@@ -424,11 +449,6 @@
     span = cols // 2
     bits = ((1, 2), (2, 1))
 
-    def flip(bit):
-        if bit == 1:
-            return chan + 1 - 2 * (chan % 2)
-        return (chan + 2) % 4
-
     diagonal = 3 - chan
 
     def is_guest(n):
@@ -468,18 +488,14 @@
     def fetch(n):
         fine_copy(n).wait_recv()
 
-    def tick(n):
-        @pl.when(is_end & leading)
-        def _():
-            fetch(n)
-            fine_copy(n).start()
-            relayout(land, fine_at(n), fine_at(n), 8)
-
-    def late(n):
-        @pl.when(is_end & jnp.logical_not(leading))
-        def _():
-            fetch(n)
-            relayout(land, fine_at(n), fine_at(n), 8)
+    def arrive(n):
+        fetch(n)
+        relayout(land, fine_at(n), fine_at(n), 8)
+
+    def share(n):
+        fetch(n)
+        fine_copy(n).start()
+        relayout(land, fine_at(n), fine_at(n), 8)
 
     def scale_and_shift(i):
         lift = lift_of(i)
@@ -559,15 +575,23 @@
     def advance(n, carry):
         active = n < count
 
-        @pl.when(n == 0)
-        def _():
-            tick(0)
-            for piece in range(tiles):
-                late(piece)
+        @pl.when(is_lead & (n == 0))
+        def _():
+            share(0)
+
+        @pl.when(is_lead & (n > 0) & active)
+        def _():
+            arrive(n)
+
+        @pl.when(is_trail & (n == 0))
+        def _():
+            arrive(0)
+            for piece in range(1, tiles):
+                share(piece)
 
         @pl.when(is_trail & active)
         def _():
-            late(tiles + n)
+            arrive(tiles + n)
 
         @pl.when(is_mid & is_guest(n))
         def _():
@@ -588,10 +612,6 @@
         def _():
             scale_and_shift(n)
 
-        @pl.when(n == 0)
-        def _():
-            tick(1)
-
         @pl.when(is_mid & (n == 0))
         def _():
             pass_on(crossed(1))
@@ -609,11 +629,6 @@
         @pl.when(n < sends)
         def _():
             start_far(n)
-
-        @pl.when(n == 0)
-        def _():
-            for piece in range(2, tiles):
-                tick(piece)
 
         @pl.when(active)
         def _():
@@ -657,16 +672,18 @@
     me = row * nchan + chan
     squares[pl.ds(me, 1), :] = jnp.sum(total, axis=0, keepdims=True)
 
+    everyone = nrows * nchan
+
     def spread(step):
-        other = (me + step) % (nrows * nchan)
-        return pltpu.make_async_remote_copy(
-            src_ref=squares.at[pl.ds(me, 1)], dst_ref=squares.at[pl.ds(me, 1)], send_sem=square_send.at[step], recv_sem=square_recv.at[step],
+        other = (me + jnp.where(side == 0, everyone - step, step)) % everyone
+        return pltpu.make_async_remote_copy(
+            src_ref=squares.at[pl.ds(me, 1)], dst_ref=squares.at[pl.ds(me, 1)], send_sem=square_send.at[step], recv_sem=square_recv.at[me],
             device_id=(other % nchan, other // nchan), device_id_type=MESH)
 
     def arrived(step):
-        other = (me + nrows * nchan - step) % (nrows * nchan)
-        return pltpu.make_async_remote_copy(
-            src_ref=squares.at[pl.ds(other, 1)], dst_ref=squares.at[pl.ds(other, 1)], send_sem=square_send.at[step], recv_sem=square_recv.at[step],
+        other = (me + step) % everyone
+        return pltpu.make_async_remote_copy(
+            src_ref=squares.at[pl.ds(other, 1)], dst_ref=squares.at[pl.ds(other, 1)], send_sem=square_send.at[step], recv_sem=square_recv.at[other],
             device_id=(other % nchan, other // nchan), device_id_type=MESH)
 
     for step in range(1, nrows * nchan):
@@ -695,7 +712,11 @@
     def _():
         for h in range(2):
             relay_half(streamed(nchips - 1), h).wait_send()
-        for n in range(tiles):
+        fine_copy(0).wait_send()
+
+    @pl.when(is_trail)
+    def _():
+        for n in range(1, tiles):
             fine_copy(n).wait_send()
 
     @pl.when(is_solver)
@@ -771,7 +792,7 @@
             pltpu.VMEM((2 * nchan, steps + 8, LANES), f32), small, pltpu.VMEM((steps, LANES), i32), pltpu.VMEM((8, LANES), i32),
             stage, stage, stage, stage, pltpu.VMEM((nrows * nchan, LANES), f32), pltpu.VMEM(((chunks + 1) * steps, 8, LANES), f32), pltpu.VMEM((3, steps, LANES), i32), small,
             pltpu.SMEM((steps, LANES), i32), pltpu.SMEM((8, LANES), i32), pltpu.SMEM((8, LANES), f32), pltpu.SMEM((3, steps, LANES), i32),
-            pltpu.SemaphoreType.REGULAR, dma((tiles,)), dma((chunks,)), dma((4,)), dma((4 * nchips,)), dma((nchips + 2,)),
+            pltpu.SemaphoreType.REGULAR((2,)), dma((tiles,)), dma((chunks,)), dma((4,)), dma((4 * nchips,)), dma((nchips + 2,)),
             dma((nchips + 2, 2)), dma((nchips + 4,)), dma((2 * tiles,)), dma((2 * tiles,)), dma((2 * tiles,)),
             dma, dma((nrows,)), dma, dma, dma((2 * nchan,)), dma((2 * nchan,)), dma((nchips,)), dma,
         ] + [dma((tiles + 2, 2))] * 6 + [dma((nrows * nchan,))] * 2 + [dma((8,))],

time: 57.7 us -> 58.1 us (level)
  no operation moved by 1% of the time
where the time goes in v6:
time: 58.1 us; the launch traced here: 57.9 us
  Pallas kernels  57.3 us (99%)
  between operations  0.64 us (1%)
    pallas_call x1, Pallas kernels, run_cycle(): pl.pallas_call(functools.partial(cycle_kernel, nchan, nrows), out_shape=(...  55.7 us
    pallas_call x1, Pallas kernels, write_outputs(): pl.pallas_call(functools.partial(write_kernel, count), out_shape=(jax.Sha...  1.55 us

profile of v6, /device:TPU:0, one launch (start us, length us, event | category | flops | bytes accessed | tf_op | source)
XLA Modules:
  0.0 57.9 jit_solution(14817505568599201838)
XLA Ops:
  0.6 55.7 %minor_cycle.1 = (f32[48,16384]{1,0:T(8,128)S(1)}, f32[48,4096]{1,0:T(8,128)S(1)}, f32[8,128]{1,0:T(8,128)S(1)}) custom-call(s32[2,32]{1,0:T(2,128)} %bitcast.1, f32[1,32,16384]{2,1,0:T(8,128)} %res.1, f32[1,256,2048]{2,1,0:T(8,128)} %psf.1), custom_call_target="tpu_custom_call" | custom-call | tf_op jit(solution)/shard_map/minor_cycle/pallas_call | solution.py:783
  56.4 1.5 %write_outputs.1 = (f32[1,32,16384]{2,1,0:T(8,128)}, f32[32,4096]{1,0:T(8,128)}) custom-call(f32[48,16384]{1,0:T(8,128)S(1)} %get-tuple-element.5.image, f32[48,4096]{1,0:T(8,128)S(1)} %get-tuple-element.6.parts, f32[8,128]{1,0:T(8,128)S(1)} %get-tuple-element.7.total), custom_call_target="tpu_custom_call" | custom-call | tf_op jit(solution)/shard_map/write_outputs/pallas_call | solution.py:822

commit v7 on v6

--- a/solution.py
+++ b/solution.py
@@ -25,7 +25,7 @@
                  first_far, first_own, passed, second, squares, changes, pair_v, sum_v, prev_s, last_s, amps_s, pair_s,
                  ready, band_sem, psf_sem, index_sem, send_sem, unit_recv, recv_sem, relay_sem, fine_send, fine_recv, fine_relay,
                  start_send, start_recv, couple_send, couple_recv, table_send, table_recv, amp_send, amp_recv,
-                 far_send, far_recv, own_send, own_recv, pass_send, pass_recv, square_send, square_recv, guest_sem):
+                 far_send, far_recv, own_send, own_recv, pass_send, pass_recv, square_send, square_recv, guest_sem, lent_send, lent_recv):
     chan, row = lax.axis_index("chan"), lax.axis_index("rows")
     chip, core = row // 2, row % 2
     partner = row + 1 - 2 * core
@@ -163,7 +163,6 @@
     is_lead, is_trail = is_end & early, is_end & jnp.logical_not(early)
     doubled = is_mid & jnp.logical_not(early)
     sends = jnp.where(is_end, jnp.where(early, tiles - 1, tiles - 2), jnp.where(early, tiles + 1, tiles + 2))
-    count = jnp.where(is_end, tiles, sends)
 
     def tile_at(i):
         return jnp.where(side == 0, i, tiles - 1 - i)
@@ -174,15 +173,23 @@
     def guest_tile(g):
         return tile_at(jnp.where(early, tiles - 1, tiles - 2 + g))
 
-    def lent(g):
-        return pltpu.make_async_remote_copy(
-            src_ref=res.at[0, tile_rows(guest_tile(g))], dst_ref=image.at[tile_rows(tiles + g)], send_sem=guest_sem.at[g], recv_sem=guest_sem.at[2 + g],
-            device_id=(chan, row + 2 - 4 * side), device_id_type=MESH)
+    head = ncols // 8
+
+    def lent(g, part):
+        width = (head, ncols - head)[part]
+        return pltpu.make_async_remote_copy(
+            src_ref=res.at[0, tile_rows(guest_tile(g)), pl.ds(head * part, width)],
+            dst_ref=image.at[tile_rows(tiles + g), pl.ds(head * part, width)],
+            send_sem=lent_send.at[g, part], recv_sem=lent_recv.at[g, part], device_id=(chan, row + 2 - 4 * side), device_id_type=MESH)
 
     def given(g):
         return pltpu.make_async_remote_copy(
-            src_ref=parts.at[tile_rows(tiles + g)], dst_ref=parts.at[tile_rows(guest_tile(g))], send_sem=guest_sem.at[4 + g], recv_sem=guest_sem.at[6 + g],
+            src_ref=parts.at[tile_rows(tiles + g)], dst_ref=parts.at[tile_rows(guest_tile(g))], send_sem=guest_sem.at[g], recv_sem=guest_sem.at[2 + g],
             device_id=(chan, row - 2 + 4 * side), device_id_type=MESH)
+
+    @pl.when(is_end)
+    def _():
+        lent(0, 0).start()
 
     for bit in (1, 2):
         pl.semaphore_signal(ready.at[0], inc=1, device_id=(flip(bit), row), device_id_type=MESH)
@@ -220,11 +227,12 @@
 
     @pl.when(is_end)
     def _():
-        lent(0).start()
+        lent(0, 1).start()
 
     @pl.when(is_trail)
     def _():
-        lent(1).start()
+        for part in range(2):
+            lent(1, part).start()
 
     @pl.when(is_root)
     def _():
@@ -573,7 +581,7 @@
     sum_v[...] = zero
 
     def advance(n, carry):
-        active = n < count
+        active = n < sends
 
         @pl.when(is_lead & (n == 0))
         def _():
@@ -595,7 +603,8 @@
 
         @pl.when(is_mid & is_guest(n))
         def _():
-            lent(n // 2).wait_recv()
+            for part in range(2):
+                lent(n // 2, part).wait_recv()
 
             def guest(b, carry):
                 work[tiles + n // 2, b] = image[tile_rows(tiles + n // 2), block_at(b)]
@@ -619,7 +628,6 @@
         @pl.when(n == sends)
         def _():
             combine(n - 1)
-            start_mine(n - 1)
 
         @pl.when(active)
         def _():
@@ -634,19 +642,15 @@
         def _():
             finish(n)
 
-        @pl.when((n == sends - 1) & (n > 1))
-        def _():
-            start_mine(n - 1)
+        @pl.when(n < sends)
+        def _():
+            start_mine(n)
 
         @pl.when((n > 0) & (n < sends))
         def _():
             combine(n - 1)
 
-        @pl.when((n == 0) | (n < sends - 2))
-        def _():
-            start_mine(n)
-
-        @pl.when(is_mid & (n == 3))
+        @pl.when(is_mid & (n == 4))
         def _():
             own(0)
             given(0).start()
@@ -688,6 +692,19 @@
 
     for step in range(1, nrows * nchan):
         spread(step).start()
+
+    def leftover(n, carry):
+        @pl.when(is_end & (n >= sends))
+        def _():
+            arrive(jnp.where(early, n, tiles + n))
+            scale_and_shift(n)
+            subtract(n)
+            finalize(n, diagonal)
+            finish(n)
+
+        return carry
+
+    lax.fori_loop(tiles - 2, tiles, leftover, 0)
 
     for s in range(2):
         @pl.when(row == roots[s])
@@ -752,12 +769,14 @@
 
     @pl.when(is_end)
     def _():
-        lent(0).wait_send()
+        for part in range(2):
+            lent(0, part).wait_send()
         given(0).wait_recv()
 
     @pl.when(is_trail)
     def _():
-        lent(1).wait_send()
+        for part in range(2):
+            lent(1, part).wait_send()
         given(1).wait_recv()
 
     for step in range(1, nrows * nchan):
@@ -795,7 +814,7 @@
             pltpu.SemaphoreType.REGULAR((2,)), dma((tiles,)), dma((chunks,)), dma((4,)), dma((4 * nchips,)), dma((nchips + 2,)),
             dma((nchips + 2, 2)), dma((nchips + 4,)), dma((2 * tiles,)), dma((2 * tiles,)), dma((2 * tiles,)),
             dma, dma((nrows,)), dma, dma, dma((2 * nchan,)), dma((2 * nchan,)), dma((nchips,)), dma,
-        ] + [dma((tiles + 2, 2))] * 6 + [dma((nrows * nchan,))] * 2 + [dma((8,))],
+        ] + [dma((tiles + 2, 2))] * 6 + [dma((nrows * nchan,))] * 2 + [dma((4,)), dma((2, 2)), dma((2, 2))],
         compiler_params=pltpu.CompilerParams(collective_id=0, has_side_effects=True, vmem_limit_bytes=VMEM - 4 * ((slab + 16) * (ncols + cols) + 8 * LANES)),
         name="minor_cycle",
     )(positions, residual, psf)

time: 58.1 us -> 56 us (0.964)
  Pallas kernels: 57.3 us -> 55.2 us
    pallas_call x1, Pallas kernels: 55.7 us -> 53.6 us  [run_cycle(): pl.pallas_call(functools.partial(cycle_kernel, nchan, nrows), out_shape=(...]
where the time goes in v7:
time: 56 us; the launch traced here: 55.8 us
  Pallas kernels  55.2 us (99%)
  between operations  0.64 us (1%)
    pallas_call x1, Pallas kernels, run_cycle(): pl.pallas_call(functools.partial(cycle_kernel, nchan, nrows), out_shape=(...  53.6 us
    pallas_call x1, Pallas kernels, write_outputs(): pl.pallas_call(functools.partial(write_kernel, count), out_shape=(jax.Sha...  1.55 us

profile of v7, /device:TPU:0, one launch (start us, length us, event | category | flops | bytes accessed | tf_op | source)
XLA Modules:
  0.0 55.8 jit_solution(18234573322733180506)
XLA Ops:
  0.6 53.6 %minor_cycle.1 = (f32[48,16384]{1,0:T(8,128)S(1)}, f32[48,4096]{1,0:T(8,128)S(1)}, f32[8,128]{1,0:T(8,128)S(1)}) custom-call(s32[2,32]{1,0:T(2,128)} %bitcast.1, f32[1,32,16384]{2,1,0:T(8,128)} %res.1, f32[1,256,2048]{2,1,0:T(8,128)} %psf.1), custom_call_target="tpu_custom_call" | custom-call | tf_op jit(solution)/shard_map/minor_cycle/pallas_call | solution.py:802
  54.3 1.5 %write_outputs.1 = (f32[1,32,16384]{2,1,0:T(8,128)}, f32[32,4096]{1,0:T(8,128)}) custom-call(f32[48,16384]{1,0:T(8,128)S(1)} %get-tuple-element.5.image, f32[48,4096]{1,0:T(8,128)S(1)} %get-tuple-element.6.parts, f32[8,128]{1,0:T(8,128)S(1)} %get-tuple-element.7.total), custom_call_target="tpu_custom_call" | custom-call | tf_op jit(solution)/shard_map/write_outputs/pallas_call | solution.py:841

commit v8 on v7

--- a/solution.py
+++ b/solution.py
@@ -173,7 +173,7 @@
     def guest_tile(g):
         return tile_at(jnp.where(early, tiles - 1, tiles - 2 + g))
 
-    head = ncols // 8
+    head = ncols // 4
 
     def lent(g, part):
         width = (head, ncols - head)[part]
@@ -642,13 +642,17 @@
         def _():
             finish(n)
 
-        @pl.when(n < sends)
+        @pl.when(is_end & (n < sends))
         def _():
             start_mine(n)
 
         @pl.when((n > 0) & (n < sends))
         def _():
             combine(n - 1)
+
+        @pl.when(is_mid & (n < sends))
+        def _():
+            start_mine(n)
 
         @pl.when(is_mid & (n == 4))
         def _():
@@ -780,11 +784,11 @@
         given(1).wait_recv()
 
     for step in range(1, nrows * nchan):
+        spread(step).wait_send()
+    for step in range(1, nrows * nchan):
         arrived(step).wait_recv()
     everything = jnp.sum(jnp.sum(squares[...], axis=0, keepdims=True), axis=1, keepdims=True)
     total_out[...] = jnp.broadcast_to(everything, total_out.shape)
-    for step in range(1, nrows * nchan):
-        spread(step).wait_send()
 
 
 def run_cycle(nchan, nrows, positions, residual, psf):

time: 56 us -> 55.9 us (level)
  no operation moved by 1% of the time
where the time goes in v8:
time: 55.9 us; the launch traced here: 55.8 us
  Pallas kernels  55.1 us (99%)
  between operations  0.64 us (1%)
    pallas_call x1, Pallas kernels, run_cycle(): pl.pallas_call(functools.partial(cycle_kernel, nchan, nrows), out_shape=(...  53.6 us
    pallas_call x1, Pallas kernels, write_outputs(): pl.pallas_call(functools.partial(write_kernel, count), out_shape=(jax.Sha...  1.55 us

profile of v8, /device:TPU:0, one launch (start us, length us, event | category | flops | bytes accessed | tf_op | source)
XLA Modules:
  0.0 55.8 jit_solution(9166688466793979685)
XLA Ops:
  0.6 53.6 %minor_cycle.1 = (f32[48,16384]{1,0:T(8,128)S(1)}, f32[48,4096]{1,0:T(8,128)S(1)}, f32[8,128]{1,0:T(8,128)S(1)}) custom-call(s32[2,32]{1,0:T(2,128)} %bitcast.1, f32[1,32,16384]{2,1,0:T(8,128)} %res.1, f32[1,256,2048]{2,1,0:T(8,128)} %psf.1), custom_call_target="tpu_custom_call" | custom-call | tf_op jit(solution)/shard_map/minor_cycle/pallas_call | solution.py:806
  54.2 1.5 %write_outputs.1 = (f32[1,32,16384]{2,1,0:T(8,128)}, f32[32,4096]{1,0:T(8,128)}) custom-call(f32[48,16384]{1,0:T(8,128)S(1)} %get-tuple-element.5.image, f32[48,4096]{1,0:T(8,128)S(1)} %get-tuple-element.6.parts, f32[8,128]{1,0:T(8,128)S(1)} %get-tuple-element.7.total), custom_call_target="tpu_custom_call" | custom-call | tf_op jit(solution)/shard_map/write_outputs/pallas_call | solution.py:845

commit v9 on v8

--- a/solution.py
+++ b/solution.py
@@ -508,9 +508,9 @@
     def scale_and_shift(i):
         lift = lift_of(i)
 
-        def eight(g, carry):
-            for n in range(8):
-                k = 8 * g + n
+        def sixteen(g, carry):
+            for n in range(16):
+                k = 16 * g + n
                 amp = amps_s[chan, k]
                 begin = lift - pos[0, k]
                 shift = (pos[1, k] - half) & (LANES - 1)
@@ -520,20 +520,20 @@
                     changes[width * k + m] = jnp.where(keep, moved[m], moved[m + 1])
             return carry
 
-        lax.fori_loop(0, steps // 8, eight, 0)
+        lax.fori_loop(0, steps // 16, sixteen, 0)
 
     def subtract(i):
         t = tile_of(i)
 
-        def eight(g, carry):
-            for n in range(8):
-                k = 8 * g + n
+        def sixteen(g, carry):
+            for n in range(16):
+                k = 16 * g + n
                 after = [work[t, prev_s[k, m]] - changes[width * k + m] for m in range(width)]
                 for m in range(width):
                     work[t, base + width * k + m] = after[m]
             return carry
 
-        lax.fori_loop(0, steps // 8, eight, 0)
+        lax.fori_loop(0, steps // 16, sixteen, 0)
 
     def finalize(i, c):
         rows = rows_at(i)
@@ -861,7 +861,7 @@
     central = slab * nrows == shard and shard * nrows == patch
     powers = all(n & (n - 1) == 0 for n in (slab, shard, patch)) and patch >= LANES
     lines = nchan == 4 and nrows == 8 and slab == 32 and ncols % (16 * LANES) == 0 and ncols <= LANES * LANES
-    if not (central and powers and lines and steps % 8 == 0 and steps <= LANES and patch < LANES * LANES):
+    if not (central and powers and lines and steps % 16 == 0 and steps <= LANES and patch < LANES * LANES):
         return on_any_device(residual, psf, positions)
     image, parts, total = run_cycle(nchan, nrows, positions.T, residual, psf)
     return write_outputs(slab * nrows * ncols, slab, image, parts, total)

time: 55.9 us -> 55.9 us (level)
  no operation moved by 1% of the time
where the time goes in v9:
time: 55.9 us; the launch traced here: 55.7 us
  Pallas kernels  55 us (98%)
  between operations  0.64 us (1%)
    pallas_call x1, Pallas kernels, run_cycle(): pl.pallas_call(functools.partial(cycle_kernel, nchan, nrows), out_shape=(...  53.5 us
    pallas_call x1, Pallas kernels, write_outputs(): pl.pallas_call(functools.partial(write_kernel, count), out_shape=(jax.Sha...  1.55 us

profile of v9, /device:TPU:0, one launch (start us, length us, event | category | flops | bytes accessed | tf_op | source)
XLA Modules:
  0.0 55.7 jit_solution(8754514682753985734)
XLA Ops:
  0.6 53.5 %minor_cycle.1 = (f32[48,16384]{1,0:T(8,128)S(1)}, f32[48,4096]{1,0:T(8,128)S(1)}, f32[8,128]{1,0:T(8,128)S(1)}) custom-call(s32[2,32]{1,0:T(2,128)} %bitcast.1, f32[1,32,16384]{2,1,0:T(8,128)} %res.1, f32[1,256,2048]{2,1,0:T(8,128)} %psf.1), custom_call_target="tpu_custom_call" | custom-call | tf_op jit(solution)/shard_map/minor_cycle/pallas_call | solution.py:806
  54.1 1.5 %write_outputs.1 = (f32[1,32,16384]{2,1,0:T(8,128)}, f32[32,4096]{1,0:T(8,128)}) custom-call(f32[48,16384]{1,0:T(8,128)S(1)} %get-tuple-element.5.image, f32[48,4096]{1,0:T(8,128)S(1)} %get-tuple-element.6.parts, f32[8,128]{1,0:T(8,128)S(1)} %get-tuple-element.7.total), custom_call_target="tpu_custom_call" | custom-call | tf_op jit(solution)/shard_map/write_outputs/pallas_call | solution.py:845
